TPU v7x, 32 devices: a whole 2x2x4 slice. The times are simulated.
32 devices in a mesh: dp: 16 (over z, x, core), rows: 2 (over y).
Axes of the slice: x: 2, y: 2, z: 4, core: 2. Of those that a mesh axis runs over, the one named last changes fastest.
Arguments:
- fine_level: bfloat16 [16, 32, 64, 256], P('dp', 'rows'), may hold values from -6 to 6
- out_grad: bfloat16 [16, 32, 64, 256], P('dp', 'rows'), may hold values from -6 to 6
- fine_input: bfloat16 [16, 32, 64, 256], P('dp', 'rows'), may hold values from -6 to 6
- mid_input: bfloat16 [16, 16, 32, 512], P('dp', None, None, 'rows'), may hold values from -6 to 6
- top_input: bfloat16 [16, 8, 16, 1024], P('dp', None, None, 'rows'), may hold values from -6 to 6
- smooth_weight: bfloat16 [3, 3, 256, 256], replicated, may hold values from -0.125 to 0.125
- fine_lateral: bfloat16 [256, 256], replicated, may hold values from -0.375 to 0.375
- mid_lateral: bfloat16 [512, 256], P('rows'), may hold values from -0.375 to 0.375
- top_lateral: bfloat16 [1024, 256], P('rows'), may hold values from -0.375 to 0.375
Outputs:
- grad_fine: bfloat16 [16, 32, 64, 256], P('dp', 'rows')
- grad_mid: bfloat16 [16, 16, 32, 512], P('dp', None, None, 'rows')
- grad_top: bfloat16 [16, 8, 16, 1024], P('dp', None, None, 'rows')
- kernel_grads: float32 [2560, 256], P('dp')
- midlat_grad: float32 [512, 256], P('rows')
- toplat_grad: float32 [1024, 256], P('rows')
All inputs are finite; a program needn't handle non-finite values.
Results may differ from a plain program's by a relative error of at most 0.0062.
Values may be sent and summed in bfloat16 or wider, within the bound.
No kernel may reach another device: no remote copies, remote signals or barrier semaphores. Data moves between devices by JAX's collectives and lax.ppermute only.
A program may use at most 64 MiB of HBM per device.

v0:
```python
import jax
import jax.numpy as jnp
from jax import lax
from jax.sharding import PartitionSpec as P


def with_halo(value, sides, width):
    for axis, dim in sides:
        count, length = (lax.axis_size(axis), value.shape[dim])
        up = [(i, (i + 1) % count) for i in range(count - 1)]
        down = [(j, i) for i, j in up]
        last = lax.slice_in_dim(value, length - width, length, axis=dim)
        leading = lax.slice_in_dim(value, 0, width, axis=dim)
        before = lax.ppermute(last, axis, up)
        after = lax.ppermute(leading, axis, down)
        value = jnp.concatenate([before, value, after], axis=dim)
    return value


def pool_two(field):
    images, rows_n, cols_n, chans = field.shape
    return field.reshape(images, rows_n // 2, 2, cols_n // 2, 2, chans).sum(axis=(2, 4))


def contract_last(left, right):
    return lax.dot_general(
        left, right, (((1,), (1,)), ((), ())), preferred_element_type=jnp.float32
    )


def contract_first(left, right):
    return lax.dot_general(
        left, right, (((0,), (0,)), ((), ())), preferred_element_type=jnp.float32
    )


def body(
    fine_level,
    out_grad,
    fine_input,
    mid_input,
    top_input,
    smooth_weight,
    fine_lateral,
    mid_lateral,
    top_lateral,
):
    images, strip, width, chans = out_grad.shape
    cells = images * strip * width
    rimmed = with_halo(out_grad, (("rows", 1),), 1)
    rimmed = jnp.pad(rimmed, ((0, 0), (0, 0), (1, 1), (0, 0)))
    fine_flat = fine_level.reshape(cells, chans)
    level_grad = jnp.zeros((cells, chans), jnp.float32)
    pieces = []
    for tap_a in range(3):
        for tap_b in range(3):
            shifted = rimmed[
                :, 2 - tap_a : 2 - tap_a + strip, 2 - tap_b : 2 - tap_b + width, :
            ].reshape(cells, chans)
            level_grad = level_grad + contract_last(shifted, smooth_weight[tap_a, tap_b])
            pieces.append(contract_first(fine_flat, shifted))
    fine_grad = level_grad.astype(jnp.bfloat16)
    grad_fine = (
        contract_last(fine_grad, fine_lateral)
        .astype(jnp.bfloat16)
        .reshape(images, strip, width, -1)
    )
    pieces.append(contract_first(fine_input.reshape(cells, -1), fine_grad))
    kernel_term = jnp.concatenate(pieces, axis=0)
    share = lax.psum_scatter(kernel_term, "dp", scatter_dimension=0, tiled=True)
    kernel_grads = lax.psum(share, "rows")
    pooled = pool_two(level_grad.reshape(images, strip, width, chans)).astype(jnp.bfloat16)
    mid_grad = lax.all_gather(pooled, "rows", axis=1, tiled=True)
    top_grad = pool_two(mid_grad.astype(jnp.float32)).astype(jnp.bfloat16)
    mid_flat = mid_grad.reshape(-1, chans)
    top_flat = top_grad.reshape(-1, chans)
    grad_mid = contract_last(mid_flat, mid_lateral).astype(jnp.bfloat16).reshape(mid_input.shape)
    grad_top = contract_last(top_flat, top_lateral).astype(jnp.bfloat16).reshape(top_input.shape)
    mid_term = contract_first(mid_input.reshape(mid_flat.shape[0], -1), mid_flat)
    top_term = contract_first(top_input.reshape(top_flat.shape[0], -1), top_flat)
    midlat_grad, toplat_grad = lax.psum((mid_term, top_term), "dp")
    return (grad_fine, grad_mid, grad_top, kernel_grads, midlat_grad, toplat_grad)


def solution(mesh):
    placed = (
        P("dp", "rows", None, None),
        P("dp", "rows", None, None),
        P("dp", "rows", None, None),
        P("dp", None, None, "rows"),
        P("dp", None, None, "rows"),
        P(),
        P(),
        P("rows", None),
        P("rows", None),
    )
    return jax.shard_map(
        body,
        mesh=mesh,
        in_specs=placed,
        out_specs=(
            P("dp", "rows", None, None),
            P("dp", None, None, "rows"),
            P("dp", None, None, "rows"),
            P("dp", None),
            P("rows", None),
            P("rows", None),
        ),
        check_vma=False,
    )
```

profile of v0, /device:TPU:0, one launch (start us, length us, event | category | flops | bytes accessed | tf_op | source)
XLA Modules:
  0.0 226.8 jit_solution(9523882617823128854)
XLA Ops:
  7.2 0.8 fusion.66
  8.1 4.9 %collective-permute-start = (bf16[1,1,64,256]{3,2,1,0:T(8,128)(2,1)S(1)}, bf16[1,1,64,256]{3,2,1,0:T(8,128)(2,1)S(1)}, u32[]{:S(2)}, u32[]{:S(2)}) collective-permute-start(bf16[1,1,64,256]{3,2,1,0:T(8,128)(2,1)S(1)} %get-tuple-element.28), channel_id=1, source_target_pairs={{0,1},{2,3},{4,5},{6,7},{8,9},{10,11},{12,13},{14,15},{16,17},{18,... | collective-permute-start | bytes 98312 | tf_op jit(solution)/shard_map/ppermute | solution.py:14
  13.0 1.3 collective-permute-start.1
  14.5 4.2 %collective-permute-done.1 = bf16[1,1,64,256]{3,2,1,0:T(8,128)(2,1)S(1)} collective-permute-done((bf16[1,1,64,256]{3,2,1,0:T(8,128)(2,1)S(1)}, bf16[1,1,64,256]{3,2,1,0:T(8,128)(2,1)S(1)}, u32[]{:S(2)}, u32[]{:S(2)}) %collective-permute-start.1) | collective-permute-done | bytes 32800 | tf_op jit(solution)/shard_map/ppermute | solution.py:15
  18.8 1.3 fusion.16
  20.1 0.5 fusion.65
  20.6 1.1 fusion.11
  21.8 1.1 fusion.10
  22.8 1.0 fusion.9
  23.9 1.1 fusion.8
  24.9 1.0 fusion.7
  26.0 1.1 fusion.6
  27.0 1.1 fusion.5
  28.1 1.1 fusion.4
  29.2 1.0 fusion.3
  33.3 0.4 copy-done.3
  33.7 1.1 fusion.2
  34.8 0.6 reshape_reshape.3
  35.4 0.9 reduce_sum.18
  36.3 5.6 %all-gather = bf16[16,32,256]{2,1,0:T(8,128)(2,1)S(1)} all-gather(bf16[8,32,256]{2,1,0:T(8,128)(2,1)S(1)} %reduce_sum.18), channel_id=2, replica_groups=mesh['dp'=16,'rows'=2] {'rows'}, dimensions={0}, use_global_device_ids=true | all-gather | bytes 393216 | tf_op jit(solution)/shard_map/all_gather | solution.py:73
  42.0 0.5 reduce.2
  42.5 1.0 convolution_bitcast_fusion
  43.6 1.0 convolution_bitcast_fusion.1
  44.6 1.0 convolution_convert_fusion.1
  45.6 1.1 convolution_convert_fusion
  46.7 52.6 %reduce-scatter.2.cloned.1.call-done = f32[160,256]{1,0:T(8,128)} async-done(((f32[2560,256]{1,0:T(8,128)}), f32[160,256]{1,0:T(8,128)}) %reduce-scatter.2.cloned.1.call-update) | async-done | bytes 163856 | tf_op jit(solution)/shard_map/reduce_scatter | solution.py:70
  99.4 0.9 convolution_convert_fusion.2
  100.3 95.1 %all-reduce.7.cloned.1.call-done = (f32[256,256]{0,1:T(8,128)}, f32[512,256]{0,1:T(8,128)}) async-done(((f32[256,256]{0,1:T(8,128)}, f32[512,256]{0,1:T(8,128)}), (f32[256,256]{0,1:T(8,128)}, f32[512,256]{0,1:T(8,128)})) %all-reduce.7.cloned.1.call-update) | async-done | bytes 786448 | tf_op jit(solution)/shard_map/psum | solution.py:81
  195.4 1.8 copy.17
  197.1 2.0 copy.18
  199.2 19.5 %all-reduce.5.cloned.1.call-done = f32[160,256]{1,0:T(8,128)} async-done(((f32[160,256]{1,0:T(8,128)}), f32[160,256]{1,0:T(8,128)}) %all-reduce.5.cloned.1.call-update) | async-done | bytes 163856 | tf_op jit(solution)/shard_map/psum | solution.py:71
  218.7 1.6 copy.31
  (35 shorter events, 3.6 us)
Async XLA Ops:
  7.2 13.4 %copy-start = (bf16[1,16,64,256]{3,2,1,0:T(8,128)(2,1)S(1)}, bf16[1,16,64,256]{3,2,1,0:T(8,128)(2,1)}, u32[]{:S(2)}) copy-start(bf16[1,16,64,256]{3,2,1,0:T(8,128)(2,1)} %param.9) | copy-start | bytes 1572868
  7.2 92.2 %reduce-scatter.2.cloned.1.call-start = ((), (), s32[]{:S(2)}) async-start(), calls=%async_computation.1 | async-start | bytes 2785280 | tf_op jit(solution)/shard_map/reduce_scatter | solution.py:70
  8.1 6.5 %collective-permute-start = (bf16[1,1,64,256]{3,2,1,0:T(8,128)(2,1)S(1)}, bf16[1,1,64,256]{3,2,1,0:T(8,128)(2,1)S(1)}, u32[]{:S(2)}, u32[]{:S(2)}) collective-permute-start(bf16[1,1,64,256]{3,2,1,0:T(8,128)(2,1)S(1)} %get-tuple-element.28), channel_id=1, source_target_pairs={{0,1},{2,3},{4,5},{6,7},{8,9},{10,11},{12,13},{14,15},{16,17},{18,... | collective-permute-start | bytes 98312 | tf_op jit(solution)/shard_map/ppermute | solution.py:14
  13.0 5.8 %collective-permute-start.1 = (bf16[1,1,64,256]{3,2,1,0:T(8,128)(2,1)S(1)}, bf16[1,1,64,256]{3,2,1,0:T(8,128)(2,1)S(1)}, u32[]{:S(2)}, u32[]{:S(2)}) collective-permute-start(bf16[1,1,64,256]{3,2,1,0:T(8,128)(2,1)S(1)} %get-tuple-element.29), channel_id=1, source_target_pairs={{1,0},{3,2},{5,4},{7,6},{9,8},{11,10},{13,12},{15,14},{17,16},{19,... | collective-permute-start | bytes 98312 | tf_op jit(solution)/shard_map/ppermute | solution.py:15
  20.0 1.7 copy-start.1
  27.0 3.2 %copy-start.2 = (bf16[3,3,256,256]{3,2,1,0:T(8,128)(2,1)S(1)}, bf16[3,3,256,256]{3,2,1,0:T(8,128)(2,1)}, u32[]{:S(2)}) copy-start(bf16[3,3,256,256]{3,2,1,0:T(8,128)(2,1)} %param.14) | copy-start | bytes 3538948
  32.6 1.0 copy-start.3
  34.7 7.8 %copy-start.8 = (bf16[1,8,16,512]{3,2,1,0:T(8,128)(2,1)S(1)}, bf16[1,8,16,512]{3,2,1,0:T(8,128)(2,1)}, u32[]{:S(2)}) copy-start(bf16[1,8,16,512]{3,2,1,0:T(8,128)(2,1)} %param.13) | copy-start | bytes 393220
  34.7 8.8 %copy-start.7 = (bf16[1,16,32,256]{3,2,1,0:T(8,128)(2,1)S(1)}, bf16[1,16,32,256]{3,2,1,0:T(8,128)(2,1)}, u32[]{:S(2)}) copy-start(bf16[1,16,32,256]{3,2,1,0:T(8,128)(2,1)} %param.12) | copy-start | bytes 786436
  34.8 160.6 %all-reduce.7.cloned.1.call-start = ((), (), s32[]{:S(2)}) async-start(), calls=%async_computation.3 | async-start | bytes 1572864 | tf_op jit(solution)/shard_map/psum | solution.py:81
  41.9 2.7 %copy-start.5 = (bf16[256,256]{1,0:T(8,128)(2,1)S(1)}, bf16[256,256]{1,0:T(8,128)(2,1)}, u32[]{:S(2)}) copy-start(bf16[256,256]{1,0:T(8,128)(2,1)} %param.16) | copy-start | bytes 393220
  42.0 3.5 %copy-start.6 = (bf16[256,256]{1,0:T(8,128)(2,1)S(1)}, bf16[256,256]{1,0:T(8,128)(2,1)}, u32[]{:S(2)}) copy-start(bf16[256,256]{1,0:T(8,128)(2,1)} %param.15) | copy-start | bytes 393220
  43.6 55.8 %copy-start.4 = (bf16[512,256]{1,0:T(8,128)(2,1)S(1)}, bf16[512,256]{1,0:T(8,128)(2,1)}, u32[]{:S(2)}) copy-start(bf16[512,256]{1,0:T(8,128)(2,1)} %param.17) | copy-start | bytes 786436
  44.6 174.2 %all-reduce.5.cloned.1.call-start = ((), (), s32[]{:S(2)}) async-start(), calls=%async_computation.2 | async-start | bytes 327680 | tf_op jit(solution)/shard_map/psum | solution.py:71
Sparse Core Ops, SparseCore 0:
  34.8 64.4 reduce-scatter.1
  103.4 91.8 all-reduce.6
  197.6 21.0 all-reduce.4
where the time goes:
time: 227 us
  waiting for transfers between devices  172 us (76%)
  matrix products  18.6 us (8%)
  between operations  13.9 us (6%)
  local copies, waits for them, and re-layouts  7.89 us (3%)
  starting transfers between devices  6.3 us (3%)
  blocking collectives  5.64 us (2%)
  other arithmetic  2.65 us (1%)
    psum x1, waiting for transfers between devices, body(): midlat_grad, toplat_grad = lax.psum((mid_term, top_term), 'dp')  95.1 us
    reduce_scatter x1, waiting for transfers between devices, body(): share = lax.psum_scatter(kernel_term, 'dp', scatter_dimension=0, tiled=True)  52.6 us
    psum x1, waiting for transfers between devices, body(): kernel_grads = lax.psum(share, 'rows')  19.5 us
    dot_general x12, matrix products, contract_first(): lax.dot_general(left, right, (((0,), (0,)), ((), ())), preferred_element_...  12.6 us
    dot_general x12, matrix products, contract_last(): lax.dot_general(left, right, (((1,), (1,)), ((), ())), preferred_element_...  5.95 us
    unnamed x21, local copies, waits for them, and re-layouts  5.82 us
    all_gather x1, blocking collectives, body(): mid_grad = lax.all_gather(pooled, 'rows', axis=1, tiled=True)  5.64 us
    ppermute x1, starting transfers between devices, with_halo(): before = lax.ppermute(last, axis, up)  4.89 us
  transfers between devices with their start and end apart: 5, of which 5 were waited for; matrix products, arithmetic and copies ran while one was open for 5% of the time, Pallas kernels for 0%

commit v1 on v0

v1 whole, which is shorter than its diff:
```python
import jax
import jax.numpy as jnp
from jax import lax
from jax.experimental import pallas as pl
from jax.experimental.pallas import tpu as pltpu
from jax.sharding import PartitionSpec as P

BF = jnp.bfloat16
F32 = jnp.float32
VMEM = pl.BlockSpec(memory_space=pltpu.VMEM)
SMEM = pl.BlockSpec(memory_space=pltpu.SMEM)


def dot_last(left, right):
    return lax.dot_general(left, right, (((1,), (1,)), ((), ())), preferred_element_type=F32)


def dot_plain(left, right):
    return lax.dot_general(left, right, (((1,), (0,)), ((), ())), preferred_element_type=F32)


def pool_rows(source, target, lines, width):
    for line in range(lines // 2):
        pair = (
            source[pl.ds(2 * line * width, width), :]
            + source[pl.ds((2 * line + 1) * width, width), :]
        )
        for part in range(target.shape[0]):
            target[part, pl.ds(line * width, width), :] = pair[:, part * 128 : (part + 1) * 128]


def pool_cols(target):
    half = target.shape[1] // 2
    return jnp.concatenate(
        [
            target[part, pl.ds(0, half, stride=2), :] + target[part, pl.ds(1, half, stride=2), :]
            for part in range(target.shape[0])
        ],
        axis=1,
    )


def split_by_core(core, term, keep, send, chunk, chips):
    for chip in range(chips):
        own = pl.multiple_of((2 * chip + core) * chunk, 8)
        other = pl.multiple_of((2 * chip + 1 - core) * chunk, 8)
        keep[pl.ds(chip * chunk, chunk), :] = term[pl.ds(own, chunk), :].astype(keep.dtype)
        send[pl.ds(chip * chunk, chunk), :] = term[pl.ds(other, chunk), :].astype(send.dtype)


def fine_kernel(width, chunk, chips):
    def run(
        core, before, grad, after, level, fine_in, weight, lateral,
        grad_fine, keep, send, pooled,
        taps, term, level_grad, pairs,
    ):
        cells, chans = grad.shape
        lines = cells // width
        column = lax.broadcasted_iota(jnp.int32, (width, chans), 0)
        for line in range(lines + 2):
            if line == 0:
                here = before[...]
            elif line == lines + 1:
                here = after[...]
            else:
                here = grad[pl.ds((line - 1) * width, width), :]
            wide = here.astype(F32)
            nxt = jnp.where(column == width - 1, 0.0, pltpu.roll(wide, width - 1, 0))
            prv = jnp.where(column == 0, 0.0, pltpu.roll(wide, 1, 0))
            at = pl.ds(line * width, width)
            taps[at, 0:chans] = nxt.astype(BF)
            taps[at, chans : 2 * chans] = here
            taps[at, 2 * chans : 3 * chans] = prv.astype(BF)
        level_t = level[...].T
        total = None
        for tap in range(3):
            shifted = taps[pl.ds((2 - tap) * width, cells), :]
            wcat = jnp.concatenate([weight[tap, b] for b in range(3)], axis=1)
            part = dot_last(shifted, wcat)
            total = part if total is None else total + part
            row = dot_plain(level_t, shifted)
            for b in range(3):
                at = pl.ds((3 * tap + b) * chans, chans)
                term[at, :] = row[:, b * chans : (b + 1) * chans]
        level_grad[...] = total
        fine = total.astype(BF)
        grad_fine[...] = dot_last(fine, lateral[...]).astype(BF)
        term[pl.ds(9 * chans, fine_in.shape[1]), :] = dot_plain(fine_in[...].T, fine)
        split_by_core(core[0], term, keep, send, chunk, chips)
        pool_rows(level_grad, pairs, lines, width)
        pooled[...] = pool_cols(pairs).astype(BF)

    return run


def coarse_kernel(width, half):
    def run(
        core, mid_grad, mid_in, top_in, mid_lat, top_lat,
        grad_mid, grad_top, keep, send,
        term, wide, pairs,
    ):
        mid = mid_grad[...]
        wide[...] = mid.astype(F32)
        grad_mid[...] = dot_last(mid, mid_lat[...]).astype(BF)
        mids = mid_in.shape[1]
        term[pl.ds(0, mids), :] = dot_plain(mid_in[...].T, mid)
        pool_rows(wide, pairs, mid.shape[0] // width, width)
        top = pool_cols(pairs).astype(BF)
        grad_top[...] = dot_last(top, top_lat[...]).astype(BF)
        term[pl.ds(mids, top_in.shape[1]), :] = dot_plain(top_in[...].T, top)
        split_by_core(core[0], term, keep, send, half, 1)

    return run


def shape(*dims, dtype=BF):
    return jax.ShapeDtypeStruct(dims, dtype)


def scratch(*dims, dtype=F32):
    return pltpu.VMEM(dims, dtype)


def pick(array, index):
    return lax.dynamic_index_in_dim(array, index, 0, keepdims=False)


def body(
    fine_level,
    out_grad,
    fine_input,
    mid_input,
    top_input,
    smooth_weight,
    fine_lateral,
    mid_lateral,
    top_lateral,
):
    images, strip, width, chans = out_grad.shape
    assert images == 1
    cells = strip * width
    spread, tall = lax.axis_size("dp"), lax.axis_size("rows")
    chips, planes = spread // 2, spread // 4
    place, row = lax.axis_index("dp"), lax.axis_index("rows")
    core, side, plane = place % 2, (place // 2) % 2, place // 4
    core_arg = core.astype(jnp.int32).reshape(1)

    up = [(i, i + 1) for i in range(tall - 1)]
    down = [(j, i) for i, j in up]
    before = lax.ppermute(out_grad[0, strip - 1], "rows", up)
    after = lax.ppermute(out_grad[0, 0], "rows", down)

    rows_all = 9 * chans + fine_input.shape[3]
    chunk = rows_all // spread
    half_rows = chips * chunk
    grad_fine, keep, send, pooled = pl.pallas_call(
        fine_kernel(width, chunk, chips),
        out_shape=(
            shape(cells, fine_input.shape[3]),
            shape(half_rows, chans, dtype=F32),
            shape(half_rows, chans),
            shape(cells // 4, chans),
        ),
        in_specs=[SMEM] + [VMEM] * 7,
        out_specs=(VMEM,) * 4,
        scratch_shapes=[
            scratch((strip + 2) * width, 3 * chans, dtype=BF),
            scratch(rows_all, chans),
            scratch(cells, chans),
            scratch(chans // 128, cells // 2, 128),
        ],
        name="fine",
    )(
        core_arg,
        before,
        out_grad.reshape(cells, chans),
        after,
        fine_level.reshape(cells, chans),
        fine_input.reshape(cells, -1),
        smooth_weight,
        fine_lateral,
    )

    def swap_core(value):
        return lax.ppermute(value, "dp", [(i, i ^ 1) for i in range(spread)])

    if tall == 2:
        other = lax.ppermute(pooled, "rows", [(0, 1), (1, 0)])
        first = row == 0
        mid_grad = jnp.concatenate(
            [jnp.where(first, pooled, other), jnp.where(first, other, pooled)], axis=0
        )
    else:
        mid_grad = lax.all_gather(pooled, "rows", axis=0, tiled=True)

    got = swap_core(send)

    mids, tops = mid_input.shape[3], top_input.shape[3]
    mid_cells = mid_grad.shape[0]
    half = (mids + tops) // 2
    grad_mid, grad_top, keep_c, send_c = pl.pallas_call(
        coarse_kernel(width // 2, half),
        out_shape=(
            shape(mid_cells, mids),
            shape(mid_cells // 4, tops),
            shape(half, chans, dtype=F32),
            shape(half, chans),
        ),
        in_specs=[SMEM] + [VMEM] * 5,
        out_specs=(VMEM,) * 4,
        scratch_shapes=[
            scratch(mids + tops, chans),
            scratch(mid_cells, chans),
            scratch(chans // 128, mid_cells // 2, 128),
        ],
        name="coarse",
    )(
        core_arg,
        mid_grad,
        mid_input.reshape(mid_cells, mids),
        top_input.reshape(mid_cells // 4, tops),
        mid_lateral,
        top_lateral,
    )
    got_c = swap_core(send_c)

    sub = chunk // tall
    both = (keep + got.astype(F32)).reshape(planes, 2, tall, sub, chans)
    both = both.transpose(1, 2, 0, 3, 4).reshape(2 * tall, planes * sub, chans)
    total = pick(both, side * tall + row)
    arrived = []
    for move_side in range(2):
        for move_row in range(tall):
            if move_side or move_row:
                block = pick(both, (side ^ move_side) * tall + (row + move_row) % tall)
                pairs = []
                for d in range(spread):
                    for r in range(tall):
                        there = (d ^ (2 * move_side)) * tall + (r + move_row) % tall
                        pairs.append((d * tall + r, there))
                arrived.append(lax.ppermute(block.astype(BF), ("dp", "rows"), pairs))
    for value in arrived:
        total = total + value.astype(F32)
    total = total.reshape(planes, sub, chans)
    share = pick(total, plane)
    arrived = []
    for move in range(1, planes):
        block = pick(total, (plane + move) % planes).astype(BF)
        pairs = [(d, (d + 4 * move) % spread) for d in range(spread)]
        arrived.append(lax.ppermute(block, "dp", pairs))
    for value in arrived:
        share = share + value.astype(F32)
    if tall == 2:
        other = lax.ppermute(share, "rows", [(0, 1), (1, 0)])
        first = row == 0
        kernel_grads = jnp.concatenate(
            [jnp.where(first, share, other), jnp.where(first, other, share)], axis=0
        )
    else:
        kernel_grads = lax.all_gather(share, "rows", axis=0, tiled=True)

    piece = half // chips
    chip = place // 2
    both = (keep_c + got_c.astype(F32)).reshape(chips, piece, chans)
    total = pick(both, chip)
    arrived = []
    for move in range(1, chips):
        block = pick(both, (chip + move) % chips).astype(BF)
        pairs = [(d, (d + 2 * move) % spread) for d in range(spread)]
        arrived.append(lax.ppermute(block, "dp", pairs))
    for value in arrived:
        total = total + value.astype(F32)
    total = total.astype(BF)
    whole = [total]
    for move in range(1, chips):
        pairs = [(d, (d + 2 * move) % spread) for d in range(spread)]
        whole.append(lax.ppermute(total, "dp", pairs))
    whole = jnp.concatenate(whole[:1] + whole[:0:-1], axis=0)
    whole = lax.dynamic_slice_in_dim(
        jnp.concatenate([whole, whole], axis=0), (chips - chip) % chips * piece, half, axis=0
    )
    other = swap_core(whole)
    first = core == 0
    coarse = jnp.concatenate(
        [jnp.where(first, whole, other), jnp.where(first, other, whole)], axis=0
    ).astype(F32)

    return (
        grad_fine.reshape(fine_input.shape),
        grad_mid.reshape(mid_input.shape),
        grad_top.reshape(top_input.shape),
        kernel_grads,
        coarse[:mids],
        coarse[mids:],
    )


def solution(mesh):
    placed = (
        P("dp", "rows", None, None),
        P("dp", "rows", None, None),
        P("dp", "rows", None, None),
        P("dp", None, None, "rows"),
        P("dp", None, None, "rows"),
        P(),
        P(),
        P("rows", None),
        P("rows", None),
    )
    return jax.shard_map(
        body,
        mesh=mesh,
        in_specs=placed,
        out_specs=(
            P("dp", "rows", None, None),
            P("dp", None, None, "rows"),
            P("dp", None, None, "rows"),
            P("dp", None),
            P("rows", None),
            P("rows", None),
        ),
        check_vma=False,
    )
```

time: 227 us -> 92.8 us (0.41)
  waiting for transfers between devices: 172 us -> 31.6 us
  starting transfers between devices: 6.3 us -> 43.7 us
  matrix products: 18.6 us -> 0 us
  between operations: 13.9 us -> 1.04 us
  Pallas kernels: 0 us -> 9.02 us
  local copies, waits for them, and re-layouts: 7.89 us -> 1.69 us
  blocking collectives: 5.64 us -> 0 us
  other arithmetic: 2.65 us -> 5.43 us
    psum x2 -> x0, waiting for transfers between devices: 115 us -> none  [the longest x1 95.1 us: body(): midlat_grad, toplat_grad = lax.psum((mid_term, top_term), 'dp')]
    reduce_scatter x1 -> x0, waiting for transfers between devices: 52.6 us -> none  [body(): share = lax.psum_scatter(kernel_term, 'dp', scatter_dimension=0, tiled=True)]
    ppermute x2 -> x27, starting transfers between devices: 6.18 us -> 43.7 us  [the longest x10 18.2 us: body(): arrived.append(lax.ppermute(block, 'dp', pairs))]
    ppermute x2 -> x27, waiting for transfers between devices: 4.51 us -> 31.6 us  [the longest x3 8 us: body(): arrived.append(lax.ppermute(block.astype(BF), ('dp', 'rows'), pairs))]
    dot_general x24 -> x0, matrix products: 18.6 us -> none  [the longest x12 12.6 us: contract_first(): lax.dot_general(left, right, (((0,), (0,)), ((), ())), preferred_element_...]
    pallas_call x0 -> x2, Pallas kernels: none -> 9.02 us  [the longest x1 6.54 us: body(): pl.pallas_call(fine_kernel(width, chunk, chips), out_shape=(shape(cells,...]
    all_gather x1 -> x0, blocking collectives: 5.64 us -> none  [body(): mid_grad = lax.all_gather(pooled, 'rows', axis=1, tiled=True)]
    unnamed x21 -> x22, local copies, waits for them, and re-layouts: 5.82 us -> 0.68 us
  transfers between devices with their start and end apart: 5 -> 27, of which waited for: 5 -> 14; matrix products, arithmetic and copies ran while one was open for 5% -> 2% of each run, Pallas kernels for 0% -> 0%
where the time goes in v1:
time: 92.8 us; the launch traced here: 92.4 us
  starting transfers between devices  43.7 us (47%)
  waiting for transfers between devices  31.6 us (34%)
  Pallas kernels  9.02 us (10%)
  other arithmetic  5.43 us (6%)
  local copies, waits for them, and re-layouts  1.69 us (2%)
  between operations  1.04 us (1%)
    ppermute x10, starting transfers between devices, body(): arrived.append(lax.ppermute(block, 'dp', pairs))  18.2 us
    ppermute x7, starting transfers between devices, body(): whole.append(lax.ppermute(total, 'dp', pairs))  11.1 us
    ppermute x3, waiting for transfers between devices, body(): arrived.append(lax.ppermute(block.astype(BF), ('dp', 'rows'), pairs))  8 us
    ppermute x7, waiting for transfers between devices, body(): whole.append(lax.ppermute(total, 'dp', pairs))  7.93 us
    ppermute x10, waiting for transfers between devices, body(): arrived.append(lax.ppermute(block, 'dp', pairs))  7.38 us
    pallas_call x1, Pallas kernels, body(): pl.pallas_call(fine_kernel(width, chunk, chips), out_shape=(shape(cells,...  6.54 us
    ppermute x1, starting transfers between devices, body(): before = lax.ppermute(out_grad[0, strip - 1], 'rows', up)  4.9 us
    ppermute x3, starting transfers between devices, body(): arrived.append(lax.ppermute(block.astype(BF), ('dp', 'rows'), pairs))  4.02 us
  transfers between devices with their start and end apart: 27, of which 14 were waited for; matrix products, arithmetic and copies ran while one was open for 2% of the time, Pallas kernels for 0%

profile of v1, /device:TPU:0, one launch (start us, length us, event | category | flops | bytes accessed | tf_op | source)
XLA Modules:
  0.0 92.4 jit_solution(12827444583759718493)
XLA Ops:
  1.4 1.3 %collective-permute-start.1 = (bf16[64,256]{1,0:T(8,128)(2,1)S(1)}, bf16[64,256]{1,0:T(8,128)(2,1)S(1)}, u32[]{:S(2)}, u32[]{:S(2)}) collective-permute-start(bf16[64,256]{1,0:T(8,128)(2,1)S(1)} %get-tuple-element.27), channel_id=1, source_target_pairs={{1,0},{3,2},{5,4},{7,6},{9,8},{11,10},{13,12},{15,14},{17,16},{19,... | collective-permute-start | bytes 98312 | tf_op jit(solution)/shard_map/ppermute | solution.py:151
  2.7 4.9 %collective-permute-start = (bf16[64,256]{1,0:T(8,128)(2,1)S(1)}, bf16[64,256]{1,0:T(8,128)(2,1)S(1)}, u32[]{:S(2)}, u32[]{:S(2)}) collective-permute-start(bf16[64,256]{1,0:T(8,128)(2,1)S(1)} %get-tuple-element.28), channel_id=1, source_target_pairs={{0,1},{2,3},{4,5},{6,7},{8,9},{10,11},{12,13},{14,15},{16,17},{18,... | collective-permute-start | bytes 98312 | tf_op jit(solution)/shard_map/ppermute | solution.py:150
  7.6 1.5 %collective-permute-done.before = bf16[64,256]{1,0:T(8,128)(2,1)S(1)} collective-permute-done((bf16[64,256]{1,0:T(8,128)(2,1)S(1)}, bf16[64,256]{1,0:T(8,128)(2,1)S(1)}, u32[]{:S(2)}, u32[]{:S(2)}) %collective-permute-start) | collective-permute-done | bytes 32800 | tf_op jit(solution)/shard_map/ppermute | solution.py:150
  9.8 6.5 %fine.1 = (bf16[1024,256]{1,0:T(8,128)(2,1)}, f32[1280,256]{1,0:T(8,128)}, bf16[1280,256]{1,0:T(8,128)(2,1)}, bf16[256,256]{1,0:T(8,128)(2,1)}) custom-call(s32[1]{0:T(128)} %bitcast.core, bf16[64,256]{1,0:T(8,128)(2,1)} %copy-done.2, bf16[1024,256]{1,0:T(8,128)(2,1)} %bitcast.81, bf16[64,256]{1,0:T(8,128)(2,1)} %copy-done.1, bf16[1024,256]{1,0:T(8,128)(2,1)} %bitcast.82, ...), custom_call_target="tpu_custom_call" | custom-call | tf_op jit(solution)/shard_map/fine/pallas_call | solution.py:156
  16.3 2.3 %collective-permute-start.2 = (bf16[256,256]{1,0:T(8,128)(2,1)}, bf16[256,256]{1,0:T(8,128)(2,1)S(1)}, u32[]{:S(2)}, u32[]{:S(2)}) collective-permute-start(bf16[256,256]{1,0:T(8,128)(2,1)} %get-tuple-element.15), channel_id=1, source_target_pairs={{0,1},{1,0},{2,3},{3,2},{4,5},{5,4},{6,7},{7,6},{8,9},{9,8},{10,11... | collective-permute-start | bytes 393224 | tf_op jit(solution)/shard_map/ppermute | solution.py:188
  18.7 3.2 %collective-permute-done.2 = bf16[256,256]{1,0:T(8,128)(2,1)S(1)} collective-permute-done((bf16[256,256]{1,0:T(8,128)(2,1)}, bf16[256,256]{1,0:T(8,128)(2,1)S(1)}, u32[]{:S(2)}, u32[]{:S(2)}) %collective-permute-start.2) | collective-permute-done | bytes 131104 | tf_op jit(solution)/shard_map/ppermute | solution.py:188
  23.5 2.5 %coarse.1 = (bf16[512,256]{1,0:T(8,128)(2,1)}, bf16[128,512]{1,0:T(8,128)(2,1)}, f32[384,256]{1,0:T(8,128)}, bf16[384,256]{1,0:T(8,128)(2,1)}) custom-call(s32[1]{0:T(128)} %bitcast.core, bf16[512,256]{1,0:T(8,128)(2,1)} %pad_maximum_fusion.1.mid_grad, bf16[512,256]{1,0:T(8,128)(2,1)} %bitcast.84, bf16[128,512]{1,0:T(8,128)(2,1)} %bitcast.85, ...), custom_call_target="tpu_custom_call" | custom-call | tf_op jit(solution)/shard_map/coarse/pallas_call | solution.py:201
  26.1 1.5 %collective-permute-done.11 = bf16[384,256]{1,0:T(8,128)(2,1)S(1)} collective-permute-done((bf16[384,256]{1,0:T(8,128)(2,1)}, bf16[384,256]{1,0:T(8,128)(2,1)S(1)}, u32[]{:S(2)}, u32[]{:S(2)}) %collective-permute-start.11) | collective-permute-done | bytes 196640 | tf_op jit(solution)/shard_map/ppermute | solution.py:185
  27.6 1.1 %convert_add_fusion.1 = f32[384,256]{1,0:T(8,128)S(1)} fusion(f32[384,256]{1,0:T(8,128)} %get-tuple-element.20, bf16[384,256]{1,0:T(8,128)(2,1)S(1)} %collective-permute-done.11), kind=kLoop, calls=%fused_computation.1 | loop fusion | flops 196608 | bytes 983040 | tf_op jit(solution)/shard_map/add | solution.py:264
  28.8 2.6 %collective-permute-start.12 = (bf16[48,256]{1,0:T(8,128)(2,1)S(1)}, bf16[48,256]{1,0:T(8,128)(2,1)S(1)}, u32[]{:S(2)}, u32[]{:S(2)}) collective-permute-start(bf16[48,256]{1,0:T(8,128)(2,1)S(1)} %get-tuple-element.31), channel_id=1, source_target_pairs={{0,4},{2,6},{4,8},{6,10},{8,12},{10,14},{12,16},{14,18},{16,20},{1... | collective-permute-start | bytes 73736 | tf_op jit(solution)/shard_map/ppermute | solution.py:270
  31.4 3.1 %collective-permute-start.18 = (bf16[48,256]{1,0:T(8,128)(2,1)S(1)}, bf16[48,256]{1,0:T(8,128)(2,1)S(1)}, u32[]{:S(2)}, u32[]{:S(2)}) collective-permute-start(bf16[48,256]{1,0:T(8,128)(2,1)S(1)} %get-tuple-element.32), channel_id=1, source_target_pairs={{0,28},{2,30},{4,0},{6,2},{8,4},{10,6},{12,8},{14,10},{16,12},{18,... | collective-permute-start | bytes 73736 | tf_op jit(solution)/shard_map/ppermute | solution.py:270
  34.6 1.9 %collective-permute-start.17 = (bf16[48,256]{1,0:T(8,128)(2,1)S(1)}, bf16[48,256]{1,0:T(8,128)(2,1)S(1)}, u32[]{:S(2)}, u32[]{:S(2)}) collective-permute-start(bf16[48,256]{1,0:T(8,128)(2,1)S(1)} %get-tuple-element.33), channel_id=1, source_target_pairs={{0,24},{2,26},{4,28},{6,30},{8,0},{10,2},{12,4},{14,6},{16,8},{18,... | collective-permute-start | bytes 73736 | tf_op jit(solution)/shard_map/ppermute | solution.py:270
  36.5 3.0 %collective-permute-start.15 = (bf16[48,256]{1,0:T(8,128)(2,1)S(1)}, bf16[48,256]{1,0:T(8,128)(2,1)S(1)}, u32[]{:S(2)}, u32[]{:S(2)}) collective-permute-start(bf16[48,256]{1,0:T(8,128)(2,1)S(1)} %get-tuple-element.35), channel_id=1, source_target_pairs={{0,16},{2,18},{4,20},{6,22},{8,24},{10,26},{12,28},{14,30},{16,0},... | collective-permute-start | bytes 73736 | tf_op jit(solution)/shard_map/ppermute | solution.py:270
  39.5 1.9 %collective-permute-start.13 = (bf16[48,256]{1,0:T(8,128)(2,1)S(1)}, bf16[48,256]{1,0:T(8,128)(2,1)S(1)}, u32[]{:S(2)}, u32[]{:S(2)}) collective-permute-start(bf16[48,256]{1,0:T(8,128)(2,1)S(1)} %get-tuple-element.37), channel_id=1, source_target_pairs={{0,8},{2,10},{4,12},{6,14},{8,16},{10,18},{12,20},{14,22},{16,24},... | collective-permute-start | bytes 73736 | tf_op jit(solution)/shard_map/ppermute | solution.py:270
  41.5 3.6 %collective-permute-done.14 = bf16[48,256]{1,0:T(8,128)(2,1)S(1)} collective-permute-done((bf16[48,256]{1,0:T(8,128)(2,1)S(1)}, bf16[48,256]{1,0:T(8,128)(2,1)S(1)}, u32[]{:S(2)}, u32[]{:S(2)}) %collective-permute-start.14) | collective-permute-done | bytes 24608 | tf_op jit(solution)/shard_map/ppermute | solution.py:270
  45.2 1.5 %collective-permute-start.19 = (bf16[48,256]{1,0:T(8,128)(2,1)S(1)}, bf16[48,256]{1,0:T(8,128)(2,1)S(1)}, u32[]{:S(2)}, u32[]{:S(2)}) collective-permute-start(bf16[48,256]{1,0:T(8,128)(2,1)S(1)} %get-tuple-element.23), channel_id=1, source_target_pairs={{0,28},{2,30},{4,0},{6,2},{8,4},{10,6},{12,8},{14,10},{16,12},{18,... | collective-permute-start | bytes 73736 | tf_op jit(solution)/shard_map/ppermute | solution.py:277
  48.2 2.5 %collective-permute-start.23 = (bf16[48,256]{1,0:T(8,128)(2,1)S(1)}, bf16[48,256]{1,0:T(8,128)(2,1)S(1)}, u32[]{:S(2)}, u32[]{:S(2)}) collective-permute-start(bf16[48,256]{1,0:T(8,128)(2,1)S(1)} %get-tuple-element.23), channel_id=1, source_target_pairs={{0,12},{2,14},{4,16},{6,18},{8,20},{10,22},{12,24},{14,26},{16,28}... | collective-permute-start | bytes 73736 | tf_op jit(solution)/shard_map/ppermute | solution.py:277
  50.7 2.1 %collective-permute-start.20 = (bf16[48,256]{1,0:T(8,128)(2,1)S(1)}, bf16[48,256]{1,0:T(8,128)(2,1)S(1)}, u32[]{:S(2)}, u32[]{:S(2)}) collective-permute-start(bf16[48,256]{1,0:T(8,128)(2,1)S(1)} %get-tuple-element.23), channel_id=1, source_target_pairs={{0,24},{2,26},{4,28},{6,30},{8,0},{10,2},{12,4},{14,6},{16,8},{18,... | collective-permute-start | bytes 73736 | tf_op jit(solution)/shard_map/ppermute | solution.py:277
  52.8 1.9 %collective-permute-done.20 = bf16[48,256]{1,0:T(8,128)(2,1)S(1)} collective-permute-done((bf16[48,256]{1,0:T(8,128)(2,1)S(1)}, bf16[48,256]{1,0:T(8,128)(2,1)S(1)}, u32[]{:S(2)}, u32[]{:S(2)}) %collective-permute-start.20) | collective-permute-done | bytes 24608 | tf_op jit(solution)/shard_map/ppermute | solution.py:277
  54.8 1.0 %collective-permute-start.21 = (bf16[48,256]{1,0:T(8,128)(2,1)S(1)}, bf16[48,256]{1,0:T(8,128)(2,1)S(1)}, u32[]{:S(2)}, u32[]{:S(2)}) collective-permute-start(bf16[48,256]{1,0:T(8,128)(2,1)S(1)} %get-tuple-element.23), channel_id=1, source_target_pairs={{0,20},{2,22},{4,24},{6,26},{8,28},{10,30},{12,0},{14,2},{16,4},{1... | collective-permute-start | bytes 73736 | tf_op jit(solution)/shard_map/ppermute | solution.py:277
  55.8 3.7 %collective-permute-done.21 = bf16[48,256]{1,0:T(8,128)(2,1)S(1)} collective-permute-done((bf16[48,256]{1,0:T(8,128)(2,1)S(1)}, bf16[48,256]{1,0:T(8,128)(2,1)S(1)}, u32[]{:S(2)}, u32[]{:S(2)}) %collective-permute-start.21) | collective-permute-done | bytes 24608 | tf_op jit(solution)/shard_map/ppermute | solution.py:277
  59.5 2.4 %collective-permute-start.22 = (bf16[48,256]{1,0:T(8,128)(2,1)S(1)}, bf16[48,256]{1,0:T(8,128)(2,1)S(1)}, u32[]{:S(2)}, u32[]{:S(2)}) collective-permute-start(bf16[48,256]{1,0:T(8,128)(2,1)S(1)} %get-tuple-element.23), channel_id=1, source_target_pairs={{0,16},{2,18},{4,20},{6,22},{8,24},{10,26},{12,28},{14,30},{16,0},... | collective-permute-start | bytes 73736 | tf_op jit(solution)/shard_map/ppermute | solution.py:277
  61.9 2.3 %collective-permute-done.22 = bf16[48,256]{1,0:T(8,128)(2,1)S(1)} collective-permute-done((bf16[48,256]{1,0:T(8,128)(2,1)S(1)}, bf16[48,256]{1,0:T(8,128)(2,1)S(1)}, u32[]{:S(2)}, u32[]{:S(2)}) %collective-permute-start.22) | collective-permute-done | bytes 24608 | tf_op jit(solution)/shard_map/ppermute | solution.py:277
  64.9 2.1 %collective-permute-start.4 = (bf16[320,256]{1,0:T(8,128)(2,1)S(1)}, bf16[320,256]{1,0:T(8,128)(2,1)S(1)}, u32[]{:S(2)}, u32[]{:S(2)}) collective-permute-start(bf16[320,256]{1,0:T(8,128)(2,1)S(1)} %get-tuple-element.24), channel_id=1, source_target_pairs={{0,1},{1,0},{2,3},{3,2},{4,5},{5,4},{6,7},{7,6},{8,9},{9,8},{10,11... | collective-permute-start | bytes 491528 | tf_op jit(solution)/shard_map/ppermute | solution.py:241
  66.9 1.4 %collective-permute-start.6 = (bf16[320,256]{1,0:T(8,128)(2,1)S(1)}, bf16[320,256]{1,0:T(8,128)(2,1)S(1)}, u32[]{:S(2)}, u32[]{:S(2)}) collective-permute-start(bf16[320,256]{1,0:T(8,128)(2,1)S(1)} %get-tuple-element.25), channel_id=1, source_target_pairs={{0,5},{1,4},{2,7},{3,6},{4,1},{5,0},{6,3},{7,2},{8,13},{9,12},{10,... | collective-permute-start | bytes 491528 | tf_op jit(solution)/shard_map/ppermute | solution.py:241
  69.0 6.3 %collective-permute-done.4 = bf16[320,256]{1,0:T(8,128)(2,1)S(1)} collective-permute-done((bf16[320,256]{1,0:T(8,128)(2,1)S(1)}, bf16[320,256]{1,0:T(8,128)(2,1)S(1)}, u32[]{:S(2)}, u32[]{:S(2)}) %collective-permute-start.4) | collective-permute-done | bytes 163872 | tf_op jit(solution)/shard_map/ppermute | solution.py:241
  75.3 1.7 %collective-permute-done.5 = bf16[320,256]{1,0:T(8,128)(2,1)S(1)} collective-permute-done((bf16[320,256]{1,0:T(8,128)(2,1)S(1)}, bf16[320,256]{1,0:T(8,128)(2,1)S(1)}, u32[]{:S(2)}, u32[]{:S(2)}) %collective-permute-start.5) | collective-permute-done | bytes 163872 | tf_op jit(solution)/shard_map/ppermute | solution.py:241
  77.1 2.8 %collective-permute-start.7 = (bf16[80,256]{1,0:T(8,128)(2,1)S(1)}, bf16[80,256]{1,0:T(8,128)(2,1)S(1)}, u32[]{:S(2)}, u32[]{:S(2)}) collective-permute-start(bf16[80,256]{1,0:T(8,128)(2,1)S(1)} %get-tuple-element.38), channel_id=1, source_target_pairs={{0,8},{2,10},{4,12},{6,14},{8,16},{10,18},{12,20},{14,22},{16,24},... | collective-permute-start | bytes 122888 | tf_op jit(solution)/shard_map/ppermute | solution.py:250
  79.9 2.4 %collective-permute-start.9 = (bf16[80,256]{1,0:T(8,128)(2,1)S(1)}, bf16[80,256]{1,0:T(8,128)(2,1)S(1)}, u32[]{:S(2)}, u32[]{:S(2)}) collective-permute-start(bf16[80,256]{1,0:T(8,128)(2,1)S(1)} %get-tuple-element.39), channel_id=1, source_target_pairs={{0,24},{2,26},{4,28},{6,30},{8,0},{10,2},{12,4},{14,6},{16,8},{18,... | collective-permute-start | bytes 122888 | tf_op jit(solution)/shard_map/ppermute | solution.py:250
  84.3 2.9 %collective-permute-done.8 = bf16[80,256]{1,0:T(8,128)(2,1)S(1)} collective-permute-done((bf16[80,256]{1,0:T(8,128)(2,1)S(1)}, bf16[80,256]{1,0:T(8,128)(2,1)S(1)}, u32[]{:S(2)}, u32[]{:S(2)}) %collective-permute-start.8) | collective-permute-done | bytes 40992 | tf_op jit(solution)/shard_map/ppermute | solution.py:250
  87.2 1.7 %collective-permute-start.10 = (f32[80,256]{1,0:T(8,128)S(1)}, f32[80,256]{1,0:T(8,128)S(1)}, u32[]{:S(2)}, u32[]{:S(2)}) collective-permute-start(f32[80,256]{1,0:T(8,128)S(1)} %fusion.7), channel_id=1, source_target_pairs={{0,1},{1,0},{2,3},{3,2},{4,5},{5,4},{6,7},{7,6},{8,9},{9,8},{10,11... | collective-permute-start | bytes 245768 | tf_op jit(solution)/shard_map/ppermute | solution.py:254
  89.7 2.1 %collective-permute-done.10 = f32[80,256]{1,0:T(8,128)S(1)} collective-permute-done((f32[80,256]{1,0:T(8,128)S(1)}, f32[80,256]{1,0:T(8,128)S(1)}, u32[]{:S(2)}, u32[]{:S(2)}) %collective-permute-start.10) | collective-permute-done | bytes 81952 | tf_op jit(solution)/shard_map/ppermute | solution.py:254
  (65 shorter events, 9.5 us)
Async XLA Ops:
  1.4 6.2 %collective-permute-start.1 = (bf16[64,256]{1,0:T(8,128)(2,1)S(1)}, bf16[64,256]{1,0:T(8,128)(2,1)S(1)}, u32[]{:S(2)}, u32[]{:S(2)}) collective-permute-start(bf16[64,256]{1,0:T(8,128)(2,1)S(1)} %get-tuple-element.27), channel_id=1, source_target_pairs={{1,0},{3,2},{5,4},{7,6},{9,8},{11,10},{13,12},{15,14},{17,16},{19,... | collective-permute-start | bytes 98312 | tf_op jit(solution)/shard_map/ppermute | solution.py:151
  2.7 6.5 %collective-permute-start = (bf16[64,256]{1,0:T(8,128)(2,1)S(1)}, bf16[64,256]{1,0:T(8,128)(2,1)S(1)}, u32[]{:S(2)}, u32[]{:S(2)}) collective-permute-start(bf16[64,256]{1,0:T(8,128)(2,1)S(1)} %get-tuple-element.28), channel_id=1, source_target_pairs={{0,1},{2,3},{4,5},{6,7},{8,9},{10,11},{12,13},{14,15},{16,17},{18,... | collective-permute-start | bytes 98312 | tf_op jit(solution)/shard_map/ppermute | solution.py:150
  7.6 1.6 %copy-start.1 = (bf16[64,256]{1,0:T(8,128)(2,1)}, bf16[64,256]{1,0:T(8,128)(2,1)S(1)}, u32[]{:S(2)}) copy-start(bf16[64,256]{1,0:T(8,128)(2,1)S(1)} %collective-permute-done.1.after) | copy-start | bytes 98308
  9.2 0.6 copy-start.2
  16.3 5.5 %collective-permute-start.2 = (bf16[256,256]{1,0:T(8,128)(2,1)}, bf16[256,256]{1,0:T(8,128)(2,1)S(1)}, u32[]{:S(2)}, u32[]{:S(2)}) collective-permute-start(bf16[256,256]{1,0:T(8,128)(2,1)} %get-tuple-element.15), channel_id=1, source_target_pairs={{0,1},{1,0},{2,3},{3,2},{4,5},{5,4},{6,7},{7,6},{8,9},{9,8},{10,11... | collective-permute-start | bytes 393224 | tf_op jit(solution)/shard_map/ppermute | solution.py:188
  25.9 20.7 %copy-start.3 = (bf16[1280,256]{1,0:T(8,128)(2,1)S(1)}, bf16[1280,256]{1,0:T(8,128)(2,1)}, u32[]{:S(2)}) copy-start(bf16[1280,256]{1,0:T(8,128)(2,1)} %get-tuple-element.19) | copy-start | bytes 1966084
  26.0 1.7 %collective-permute-start.11 = (bf16[384,256]{1,0:T(8,128)(2,1)}, bf16[384,256]{1,0:T(8,128)(2,1)S(1)}, u32[]{:S(2)}, u32[]{:S(2)}) collective-permute-start(bf16[384,256]{1,0:T(8,128)(2,1)} %get-tuple-element.21), channel_id=1, source_target_pairs={{0,2},{2,0},{4,6},{6,4},{8,10},{10,8},{12,14},{14,12},{16,18},{18,... | collective-permute-start | bytes 589832 | tf_op jit(solution)/shard_map/ppermute | solution.py:185
  27.6 36.9 %copy-start = (f32[1280,256]{1,0:T(8,128)S(1)}, f32[1280,256]{1,0:T(8,128)}, u32[]{:S(2)}) copy-start(f32[1280,256]{1,0:T(8,128)} %get-tuple-element.18) | copy-start | bytes 3932164
  28.8 10.7 %collective-permute-start.12 = (bf16[48,256]{1,0:T(8,128)(2,1)S(1)}, bf16[48,256]{1,0:T(8,128)(2,1)S(1)}, u32[]{:S(2)}, u32[]{:S(2)}) collective-permute-start(bf16[48,256]{1,0:T(8,128)(2,1)S(1)} %get-tuple-element.31), channel_id=1, source_target_pairs={{0,4},{2,6},{4,8},{6,10},{8,12},{10,14},{12,16},{14,18},{16,20},{1... | collective-permute-start | bytes 73736 | tf_op jit(solution)/shard_map/ppermute | solution.py:270
  31.4 8.0 %collective-permute-start.18 = (bf16[48,256]{1,0:T(8,128)(2,1)S(1)}, bf16[48,256]{1,0:T(8,128)(2,1)S(1)}, u32[]{:S(2)}, u32[]{:S(2)}) collective-permute-start(bf16[48,256]{1,0:T(8,128)(2,1)S(1)} %get-tuple-element.32), channel_id=1, source_target_pairs={{0,28},{2,30},{4,0},{6,2},{8,4},{10,6},{12,8},{14,10},{16,12},{18,... | collective-permute-start | bytes 73736 | tf_op jit(solution)/shard_map/ppermute | solution.py:270
  34.6 6.8 %collective-permute-start.17 = (bf16[48,256]{1,0:T(8,128)(2,1)S(1)}, bf16[48,256]{1,0:T(8,128)(2,1)S(1)}, u32[]{:S(2)}, u32[]{:S(2)}) collective-permute-start(bf16[48,256]{1,0:T(8,128)(2,1)S(1)} %get-tuple-element.33), channel_id=1, source_target_pairs={{0,24},{2,26},{4,28},{6,30},{8,0},{10,2},{12,4},{14,6},{16,8},{18,... | collective-permute-start | bytes 73736 | tf_op jit(solution)/shard_map/ppermute | solution.py:270
  36.5 4.9 %collective-permute-start.16 = (bf16[48,256]{1,0:T(8,128)(2,1)S(1)}, bf16[48,256]{1,0:T(8,128)(2,1)S(1)}, u32[]{:S(2)}, u32[]{:S(2)}) collective-permute-start(bf16[48,256]{1,0:T(8,128)(2,1)S(1)} %get-tuple-element.34), channel_id=1, source_target_pairs={{0,20},{2,22},{4,24},{6,26},{8,28},{10,30},{12,0},{14,2},{16,4},{1... | collective-permute-start | bytes 73736 | tf_op jit(solution)/shard_map/ppermute | solution.py:270
  36.5 5.0 %collective-permute-start.15 = (bf16[48,256]{1,0:T(8,128)(2,1)S(1)}, bf16[48,256]{1,0:T(8,128)(2,1)S(1)}, u32[]{:S(2)}, u32[]{:S(2)}) collective-permute-start(bf16[48,256]{1,0:T(8,128)(2,1)S(1)} %get-tuple-element.35), channel_id=1, source_target_pairs={{0,16},{2,18},{4,20},{6,22},{8,24},{10,26},{12,28},{14,30},{16,0},... | collective-permute-start | bytes 73736 | tf_op jit(solution)/shard_map/ppermute | solution.py:270
  39.4 5.6 %collective-permute-start.14 = (bf16[48,256]{1,0:T(8,128)(2,1)S(1)}, bf16[48,256]{1,0:T(8,128)(2,1)S(1)}, u32[]{:S(2)}, u32[]{:S(2)}) collective-permute-start(bf16[48,256]{1,0:T(8,128)(2,1)S(1)} %get-tuple-element.36), channel_id=1, source_target_pairs={{0,12},{2,14},{4,16},{6,18},{8,20},{10,22},{12,24},{14,26},{16,28}... | collective-permute-start | bytes 73736 | tf_op jit(solution)/shard_map/ppermute | solution.py:270
  39.5 5.7 %collective-permute-start.13 = (bf16[48,256]{1,0:T(8,128)(2,1)S(1)}, bf16[48,256]{1,0:T(8,128)(2,1)S(1)}, u32[]{:S(2)}, u32[]{:S(2)}) collective-permute-start(bf16[48,256]{1,0:T(8,128)(2,1)S(1)} %get-tuple-element.37), channel_id=1, source_target_pairs={{0,8},{2,10},{4,12},{6,14},{8,16},{10,18},{12,20},{14,22},{16,24},... | collective-permute-start | bytes 73736 | tf_op jit(solution)/shard_map/ppermute | solution.py:270
  45.2 5.5 %collective-permute-start.19 = (bf16[48,256]{1,0:T(8,128)(2,1)S(1)}, bf16[48,256]{1,0:T(8,128)(2,1)S(1)}, u32[]{:S(2)}, u32[]{:S(2)}) collective-permute-start(bf16[48,256]{1,0:T(8,128)(2,1)S(1)} %get-tuple-element.23), channel_id=1, source_target_pairs={{0,28},{2,30},{4,0},{6,2},{8,4},{10,6},{12,8},{14,10},{16,12},{18,... | collective-permute-start | bytes 73736 | tf_op jit(solution)/shard_map/ppermute | solution.py:277
  46.6 17.9 %collective-permute-start.3 = (bf16[1280,256]{1,0:T(8,128)(2,1)S(1)}, bf16[1280,256]{1,0:T(8,128)(2,1)S(1)}, u32[]{:S(2)}, u32[]{:S(2)}) collective-permute-start(bf16[1280,256]{1,0:T(8,128)(2,1)S(1)} %copy-done.3), channel_id=1, source_target_pairs={{0,2},{2,0},{4,6},{6,4},{8,10},{10,8},{12,14},{14,12},{16,18},{18,... | collective-permute-start | bytes 1966088 | tf_op jit(solution)/shard_map/ppermute | solution.py:185
  46.6 17.6 %collective-permute-start.25 = (bf16[48,256]{1,0:T(8,128)(2,1)S(1)}, bf16[48,256]{1,0:T(8,128)(2,1)S(1)}, u32[]{:S(2)}, u32[]{:S(2)}) collective-permute-start(bf16[48,256]{1,0:T(8,128)(2,1)S(1)} %get-tuple-element.23), channel_id=1, source_target_pairs={{0,4},{2,6},{4,8},{6,10},{8,12},{10,14},{12,16},{14,18},{16,20},{1... | collective-permute-start | bytes 73736 | tf_op jit(solution)/shard_map/ppermute | solution.py:277
  47.3 17.0 %collective-permute-start.24 = (bf16[48,256]{1,0:T(8,128)(2,1)S(1)}, bf16[48,256]{1,0:T(8,128)(2,1)S(1)}, u32[]{:S(2)}, u32[]{:S(2)}) collective-permute-start(bf16[48,256]{1,0:T(8,128)(2,1)S(1)} %get-tuple-element.23), channel_id=1, source_target_pairs={{0,8},{2,10},{4,12},{6,14},{8,16},{10,18},{12,20},{14,22},{16,24},... | collective-permute-start | bytes 73736 | tf_op jit(solution)/shard_map/ppermute | solution.py:277
  48.2 16.1 %collective-permute-start.23 = (bf16[48,256]{1,0:T(8,128)(2,1)S(1)}, bf16[48,256]{1,0:T(8,128)(2,1)S(1)}, u32[]{:S(2)}, u32[]{:S(2)}) collective-permute-start(bf16[48,256]{1,0:T(8,128)(2,1)S(1)} %get-tuple-element.23), channel_id=1, source_target_pairs={{0,12},{2,14},{4,16},{6,18},{8,20},{10,22},{12,24},{14,26},{16,28}... | collective-permute-start | bytes 73736 | tf_op jit(solution)/shard_map/ppermute | solution.py:277
  50.7 4.1 %collective-permute-start.20 = (bf16[48,256]{1,0:T(8,128)(2,1)S(1)}, bf16[48,256]{1,0:T(8,128)(2,1)S(1)}, u32[]{:S(2)}, u32[]{:S(2)}) collective-permute-start(bf16[48,256]{1,0:T(8,128)(2,1)S(1)} %get-tuple-element.23), channel_id=1, source_target_pairs={{0,24},{2,26},{4,28},{6,30},{8,0},{10,2},{12,4},{14,6},{16,8},{18,... | collective-permute-start | bytes 73736 | tf_op jit(solution)/shard_map/ppermute | solution.py:277
  54.8 4.7 %collective-permute-start.21 = (bf16[48,256]{1,0:T(8,128)(2,1)S(1)}, bf16[48,256]{1,0:T(8,128)(2,1)S(1)}, u32[]{:S(2)}, u32[]{:S(2)}) collective-permute-start(bf16[48,256]{1,0:T(8,128)(2,1)S(1)} %get-tuple-element.23), channel_id=1, source_target_pairs={{0,20},{2,22},{4,24},{6,26},{8,28},{10,30},{12,0},{14,2},{16,4},{1... | collective-permute-start | bytes 73736 | tf_op jit(solution)/shard_map/ppermute | solution.py:277
  59.5 4.7 %collective-permute-start.22 = (bf16[48,256]{1,0:T(8,128)(2,1)S(1)}, bf16[48,256]{1,0:T(8,128)(2,1)S(1)}, u32[]{:S(2)}, u32[]{:S(2)}) collective-permute-start(bf16[48,256]{1,0:T(8,128)(2,1)S(1)} %get-tuple-element.23), channel_id=1, source_target_pairs={{0,16},{2,18},{4,20},{6,22},{8,24},{10,26},{12,28},{14,30},{16,0},... | collective-permute-start | bytes 73736 | tf_op jit(solution)/shard_map/ppermute | solution.py:277
  64.4 4.5 %collective-permute-start.26 = (bf16[384,256]{1,0:T(8,128)(2,1)S(1)}, bf16[384,256]{1,0:T(8,128)(2,1)S(1)}, u32[]{:S(2)}, u32[]{:S(2)}) collective-permute-start(bf16[384,256]{1,0:T(8,128)(2,1)S(1)} %constant_dynamic-slice_fusion), channel_id=1, source_target_pairs={{0,2},{2,0},{4,6},{6,4},{8,10},{10,8},{12,14},{14,12},{16,18},{18,... | collective-permute-start | bytes 589832 | tf_op jit(solution)/shard_map/ppermute | solution.py:185
  64.9 10.4 %collective-permute-start.4 = (bf16[320,256]{1,0:T(8,128)(2,1)S(1)}, bf16[320,256]{1,0:T(8,128)(2,1)S(1)}, u32[]{:S(2)}, u32[]{:S(2)}) collective-permute-start(bf16[320,256]{1,0:T(8,128)(2,1)S(1)} %get-tuple-element.24), channel_id=1, source_target_pairs={{0,1},{1,0},{2,3},{3,2},{4,5},{5,4},{6,7},{7,6},{8,9},{9,8},{10,11... | collective-permute-start | bytes 491528 | tf_op jit(solution)/shard_map/ppermute | solution.py:241
  66.9 8.4 %collective-permute-start.6 = (bf16[320,256]{1,0:T(8,128)(2,1)S(1)}, bf16[320,256]{1,0:T(8,128)(2,1)S(1)}, u32[]{:S(2)}, u32[]{:S(2)}) collective-permute-start(bf16[320,256]{1,0:T(8,128)(2,1)S(1)} %get-tuple-element.25), channel_id=1, source_target_pairs={{0,5},{1,4},{2,7},{3,6},{4,1},{5,0},{6,3},{7,2},{8,13},{9,12},{10,... | collective-permute-start | bytes 491528 | tf_op jit(solution)/shard_map/ppermute | solution.py:241
  68.4 8.6 %collective-permute-start.5 = (bf16[320,256]{1,0:T(8,128)(2,1)S(1)}, bf16[320,256]{1,0:T(8,128)(2,1)S(1)}, u32[]{:S(2)}, u32[]{:S(2)}) collective-permute-start(bf16[320,256]{1,0:T(8,128)(2,1)S(1)} %get-tuple-element.26), channel_id=1, source_target_pairs={{0,4},{1,5},{2,6},{3,7},{4,0},{5,1},{6,2},{7,3},{8,12},{9,13},{10,... | collective-permute-start | bytes 491528 | tf_op jit(solution)/shard_map/ppermute | solution.py:241
  77.1 7.2 %collective-permute-start.7 = (bf16[80,256]{1,0:T(8,128)(2,1)S(1)}, bf16[80,256]{1,0:T(8,128)(2,1)S(1)}, u32[]{:S(2)}, u32[]{:S(2)}) collective-permute-start(bf16[80,256]{1,0:T(8,128)(2,1)S(1)} %get-tuple-element.38), channel_id=1, source_target_pairs={{0,8},{2,10},{4,12},{6,14},{8,16},{10,18},{12,20},{14,22},{16,24},... | collective-permute-start | bytes 122888 | tf_op jit(solution)/shard_map/ppermute | solution.py:250
  79.9 4.4 %collective-permute-start.9 = (bf16[80,256]{1,0:T(8,128)(2,1)S(1)}, bf16[80,256]{1,0:T(8,128)(2,1)S(1)}, u32[]{:S(2)}, u32[]{:S(2)}) collective-permute-start(bf16[80,256]{1,0:T(8,128)(2,1)S(1)} %get-tuple-element.39), channel_id=1, source_target_pairs={{0,24},{2,26},{4,28},{6,30},{8,0},{10,2},{12,4},{14,6},{16,8},{18,... | collective-permute-start | bytes 122888 | tf_op jit(solution)/shard_map/ppermute | solution.py:250
  82.3 4.9 %collective-permute-start.8 = (bf16[80,256]{1,0:T(8,128)(2,1)S(1)}, bf16[80,256]{1,0:T(8,128)(2,1)S(1)}, u32[]{:S(2)}, u32[]{:S(2)}) collective-permute-start(bf16[80,256]{1,0:T(8,128)(2,1)S(1)} %get-tuple-element.40), channel_id=1, source_target_pairs={{0,16},{2,18},{4,20},{6,22},{8,24},{10,26},{12,28},{14,30},{16,0},... | collective-permute-start | bytes 122888 | tf_op jit(solution)/shard_map/ppermute | solution.py:250
  87.2 4.5 %collective-permute-start.10 = (f32[80,256]{1,0:T(8,128)S(1)}, f32[80,256]{1,0:T(8,128)S(1)}, u32[]{:S(2)}, u32[]{:S(2)}) collective-permute-start(f32[80,256]{1,0:T(8,128)S(1)} %fusion.7), channel_id=1, source_target_pairs={{0,1},{1,0},{2,3},{3,2},{4,5},{5,4},{6,7},{7,6},{8,9},{9,8},{10,11... | collective-permute-start | bytes 245768 | tf_op jit(solution)/shard_map/ppermute | solution.py:254

commit v2 on v0

v2 whole, which is shorter than its diff:
```python
import jax
import jax.numpy as jnp
from jax import lax
from jax.experimental import pallas as pl
from jax.experimental.pallas import tpu as pltpu
from jax.sharding import PartitionSpec as P


BF = jnp.bfloat16
F32 = jnp.float32
VMEM = pl.BlockSpec(memory_space=pltpu.VMEM)
SMEM = pl.BlockSpec(memory_space=pltpu.SMEM)


def dot_last(left, right):
    return lax.dot_general(left, right, (((1,), (1,)), ((), ())), preferred_element_type=F32)


def dot_plain(left, right):
    return lax.dot_general(left, right, (((1,), (0,)), ((), ())), preferred_element_type=F32)


def pool_rows(source, target, lines, width):
    for line in range(lines // 2):
        pair = (
            source[pl.ds(2 * line * width, width), :]
            + source[pl.ds((2 * line + 1) * width, width), :]
        )
        for part in range(target.shape[0]):
            target[part, pl.ds(line * width, width), :] = pair[:, part * 128 : (part + 1) * 128]


def pool_cols(target):
    half = target.shape[1] // 2
    return jnp.concatenate(
        [
            target[part, pl.ds(0, half, stride=2), :] + target[part, pl.ds(1, half, stride=2), :]
            for part in range(target.shape[0])
        ],
        axis=1,
    )


def level_kernel(width):
    def run(place, before, grad, after, weight, taps, fine, pooled, level_grad, pairs):
        cells, chans = grad.shape
        lines = cells // width
        column = lax.broadcasted_iota(jnp.int32, (width, chans), 0)
        for line in range(lines + 2):
            if line == 0:
                here = jnp.where(place[1] > 0, before[...].astype(F32), 0.0)
            elif line == lines + 1:
                here = jnp.where(place[2] > 0, after[...].astype(F32), 0.0)
            else:
                here = grad[pl.ds((line - 1) * width, width), :].astype(F32)
            nxt = jnp.where(column == width - 1, 0.0, pltpu.roll(here, width - 1, 0))
            prv = jnp.where(column == 0, 0.0, pltpu.roll(here, 1, 0))
            at = pl.ds(line * width, width)
            taps[at, 0:chans] = nxt.astype(BF)
            taps[at, chans : 2 * chans] = here.astype(BF)
            taps[at, 2 * chans : 3 * chans] = prv.astype(BF)
        total = None
        for tap in range(3):
            shifted = taps[pl.ds((2 - tap) * width, cells), :]
            wcat = jnp.concatenate([weight[tap, b] for b in range(3)], axis=1)
            part = dot_last(shifted, wcat)
            total = part if total is None else total + part
        level_grad[...] = total
        fine[...] = total.astype(BF)
        pool_rows(level_grad, pairs, lines, width)
        pooled[...] = pool_cols(pairs).astype(BF)

    return run


def weight_kernel(width, chips, tall, sub):
    def run(place, taps, fine, level, fine_in, *refs):
        term = refs[-1]
        cells, chans = fine.shape
        level_t = level[...].T
        for tap in range(3):
            row = dot_plain(level_t, taps[pl.ds((2 - tap) * width, cells), :])
            for b in range(3):
                at = pl.ds((3 * tap + b) * chans, chans)
                term[at, :] = row[:, b * chans : (b + 1) * chans]
        term[pl.ds(9 * chans, fine_in.shape[1]), :] = dot_plain(fine_in[...].T, fine[...])
        if len(refs) == 1:
            return
        keep, send = refs[:2]
        core = place[0]
        for chip in range(chips):
            for part in range(tall):
                to = pl.ds((part * chips + chip) * sub, sub)
                own = pl.multiple_of(((2 * chip + core) * tall + part) * sub, 8)
                other = pl.multiple_of(((2 * chip + 1 - core) * tall + part) * sub, 8)
                keep[to, :] = term[pl.ds(own, sub), :]
                send[to, :] = term[pl.ds(other, sub), :].astype(BF)

    return run


def grads_kernel(fine, mid, top, fine_lat, mid_lat, top_lat, grad_fine, grad_mid, grad_top):
    grad_fine[...] = dot_last(fine[...], fine_lat[...]).astype(BF)
    grad_mid[...] = dot_last(mid[...], mid_lat[...]).astype(BF)
    grad_top[...] = dot_last(top[...], top_lat[...]).astype(BF)


def coarse_kernel(width, half, blocks):
    def run(place, *refs):
        parts, (mid_in, top_in) = refs[:blocks], refs[blocks : blocks + 2]
        whole, top_out, keep, send, term, wide, pairs = refs[blocks + 2 :]
        count = parts[0].shape[0]
        spots = (place[3], 1 - place[3]) if blocks == 2 else (0,)
        for part, at in zip(parts, spots):
            whole[pl.ds(pl.multiple_of(at * count, 16), count), :] = part[...]
        mid = whole[...]
        wide[...] = mid.astype(F32)
        mids = mid_in.shape[1]
        term[pl.ds(0, mids), :] = dot_plain(mid_in[...].T, mid)
        pool_rows(wide, pairs, mid.shape[0] // width, width)
        top = pool_cols(pairs).astype(BF)
        top_out[...] = top
        term[pl.ds(mids, top_in.shape[1]), :] = dot_plain(top_in[...].T, top)
        core = place[0]
        own, other = pl.multiple_of(core * half, 8), pl.multiple_of((1 - core) * half, 8)
        keep[...] = term[pl.ds(own, half), :]
        send[...] = term[pl.ds(other, half), :].astype(BF)

    return run


def shape(*dims, dtype=BF):
    return jax.ShapeDtypeStruct(dims, dtype)


def scratch(*dims, dtype=F32):
    return pltpu.VMEM(dims, dtype)


def cost(flops):
    return pl.CostEstimate(flops=flops, bytes_accessed=0, transcendentals=0)


def pick(array, index):
    return lax.dynamic_index_in_dim(array, index, 0, keepdims=False)


def work(
    fine_level,
    out_grad,
    fine_input,
    mid_input,
    top_input,
    smooth_weight,
    fine_lateral,
    mid_lateral,
    top_lateral,
):
    images, strip, width, chans = out_grad.shape
    assert images == 1
    cells = strip * width
    spread, tall = lax.axis_size("dp"), lax.axis_size("rows")
    place, row = lax.axis_index("dp"), lax.axis_index("rows")
    core = place % 2
    chips = spread // 2
    there = jnp.stack([core, row > 0, row < tall - 1, row]).astype(jnp.int32)
    swap = [(0, 1), (1, 0)]

    def swap_core(value):
        return lax.ppermute(value, "dp", [(i, i ^ 1) for i in range(spread)])

    def join(index, mine, other):
        first = index == 0
        return jnp.concatenate(
            [jnp.where(first, mine, other), jnp.where(first, other, mine)], axis=0
        )

    flat = out_grad.reshape(cells, chans)
    top_line, low_line = flat[:width], flat[cells - width :]
    if tall == 2:
        before = after = lax.ppermute(jnp.where(row == 0, low_line, top_line), "rows", swap)
    else:
        up = [(i, i + 1) for i in range(tall - 1)]
        before = lax.ppermute(low_line, "rows", up)
        after = lax.ppermute(top_line, "rows", [(j, i) for i, j in up])

    taps, fine, pooled = pl.pallas_call(
        level_kernel(width),
        out_shape=(
            shape((strip + 2) * width, 3 * chans),
            shape(cells, chans),
            shape(cells // 4, chans),
        ),
        in_specs=[SMEM] + [VMEM] * 4,
        out_specs=(VMEM,) * 3,
        scratch_shapes=[scratch(cells, chans), scratch(chans // 128, cells // 2, 128)],
        cost_estimate=cost(18 * cells * chans * chans),
        name="level",
    )(there, before, flat, after, smooth_weight)

    if tall == 2:
        blocks = (pooled, lax.ppermute(pooled, "rows", swap))
    else:
        blocks = (lax.all_gather(pooled, "rows", axis=0, tiled=True),)

    rows_all = 9 * chans + fine_input.shape[3]
    sub = rows_all // (spread * tall)
    half_rows = rows_all // 2
    aligned = sub % 8 == 0
    whole_term = shape(rows_all, chans, dtype=F32)
    halves = (shape(half_rows, chans, dtype=F32), shape(half_rows, chans))
    out = pl.pallas_call(
        weight_kernel(width, chips, tall, sub),
        out_shape=halves if aligned else (whole_term,),
        in_specs=[SMEM] + [VMEM] * 4,
        out_specs=(VMEM,) * (2 if aligned else 1),
        scratch_shapes=[scratch(rows_all, chans)] if aligned else [],
        cost_estimate=cost(20 * cells * chans * chans),
        name="weights",
    )(
        there,
        taps,
        fine,
        fine_level.reshape(cells, chans),
        fine_input.reshape(cells, -1),
    )
    if aligned:
        keep, send = out
    else:
        term = out[0].reshape(chips, 2, tall, sub, chans).transpose(1, 2, 0, 3, 4)
        term = term.reshape(2, half_rows, chans)
        keep, send = pick(term, core), pick(term, 1 - core).astype(BF)
    got = swap_core(send)

    both = (keep + got.astype(F32)).reshape(tall, chips * sub, chans)
    fine_sum = pick(both, row)
    for move in range(1, tall):
        block = pick(both, (row + move) % tall).astype(BF)
        pairs = [(r, (r + move) % tall) for r in range(tall)]
        moved = lax.ppermute(block, "rows", pairs)
        fine_sum = fine_sum + moved.astype(F32)

    mids, tops = mid_input.shape[3], top_input.shape[3]
    mid_cells = mid_input.shape[1] * mid_input.shape[2]
    half = (mids + tops) // 2
    mid_grad, top_grad, keep, send = pl.pallas_call(
        coarse_kernel(width // 2, half, len(blocks)),
        out_shape=(
            shape(mid_cells, chans),
            shape(mid_cells // 4, chans),
            shape(half, chans, dtype=F32),
            shape(half, chans),
        ),
        in_specs=[SMEM] + [VMEM] * (2 + len(blocks)),
        out_specs=(VMEM,) * 4,
        scratch_shapes=[
            scratch(mids + tops, chans),
            scratch(mid_cells, chans),
            scratch(chans // 128, mid_cells // 2, 128),
        ],
        cost_estimate=cost(2 * mid_cells * chans * (mids + tops // 4)),
        name="coarse",
    )(there, *blocks, mid_input.reshape(mid_cells, mids), top_input.reshape(mid_cells // 4, tops))
    coarse_sum = keep + swap_core(send).astype(F32)

    grad_fine, grad_mid, grad_top = pl.pallas_call(
        grads_kernel,
        out_shape=(
            shape(cells, fine_input.shape[3]),
            shape(mid_cells, mids),
            shape(mid_cells // 4, tops),
        ),
        in_specs=[VMEM] * 6,
        out_specs=(VMEM,) * 3,
        cost_estimate=cost(4 * cells * chans * chans),
        name="grads",
    )(fine, mid_grad, top_grad, fine_lateral, mid_lateral, top_lateral)

    piece = half // chips
    groups = [[2 * k + c for k in range(chips)] for c in range(2)]
    packed = jnp.concatenate(
        [
            fine_sum.reshape(chips, sub, chans).astype(BF),
            coarse_sum.reshape(chips, piece, chans).astype(BF),
        ],
        axis=1,
    )
    packed = lax.all_to_all(packed, "dp", 0, 0, tiled=True, axis_index_groups=groups)
    share = packed[:, :sub].astype(F32).sum(axis=0)
    part = packed[:, sub:].astype(F32).sum(axis=0).astype(BF)

    if tall == 2:
        kernel_grads = join(row, share, lax.ppermute(share, "rows", swap))
    else:
        kernel_grads = lax.all_gather(share, "rows", axis=0, tiled=True)

    part = jnp.broadcast_to(part[None], (chips, piece, chans))
    part = lax.all_to_all(part, "dp", 0, 0, tiled=True, axis_index_groups=groups)
    part = part.reshape(half, chans)
    coarse = join(core, part, swap_core(part)).astype(F32)

    return (
        grad_fine.reshape(fine_input.shape),
        grad_mid.reshape(mid_input.shape),
        grad_top.reshape(top_input.shape),
        kernel_grads,
        coarse[:mids],
        coarse[mids:],
    )


def solution(mesh):
    placed = (
        P("dp", "rows", None, None),
        P("dp", "rows", None, None),
        P("dp", "rows", None, None),
        P("dp", None, None, "rows"),
        P("dp", None, None, "rows"),
        P(),
        P(),
        P("rows", None),
        P("rows", None),
    )
    return jax.shard_map(
        work,
        mesh=mesh,
        in_specs=placed,
        out_specs=(
            P("dp", "rows", None, None),
            P("dp", None, None, "rows"),
            P("dp", None, None, "rows"),
            P("dp", None),
            P("rows", None),
            P("rows", None),
        ),
        check_vma=False,
    )
```

time: 227 us -> 72.7 us (0.32)
  waiting for transfers between devices: 172 us -> 18 us
  matrix products: 18.6 us -> 0 us
  blocking collectives: 5.64 us -> 20.1 us
  Pallas kernels: 0 us -> 13.9 us
  between operations: 13.9 us -> 0.71 us
  local copies, waits for them, and re-layouts: 7.89 us -> 2.01 us
  starting transfers between devices: 6.3 us -> 12.1 us
  other arithmetic: 2.65 us -> 5.38 us
    psum x2 -> x0, waiting for transfers between devices: 115 us -> none  [the longest x1 95.1 us: body(): midlat_grad, toplat_grad = lax.psum((mid_term, top_term), 'dp')]
    reduce_scatter x1 -> x0, waiting for transfers between devices: 52.6 us -> none  [body(): share = lax.psum_scatter(kernel_term, 'dp', scatter_dimension=0, tiled=True)]
    all_to_all x0 -> x1, blocking collectives: none -> 20.1 us  [work(): lax.all_to_all(packed, 'dp', 0, 0, tiled=True, axis_index_groups=groups)]
    dot_general x24 -> x0, matrix products: 18.6 us -> none  [the longest x12 12.6 us: contract_first(): lax.dot_general(left, right, (((0,), (0,)), ((), ())), preferred_element_...]
    pallas_call x0 -> x4, Pallas kernels: none -> 13.9 us  [the longest x1 4.84 us: work(): pl.pallas_call(weight_kernel(width, chips, tall, sub), out_shape=halves i...]
    ppermute x2 -> x7, waiting for transfers between devices: 4.51 us -> 14.5 us  [the longest x1 8.32 us: work(): moved = lax.ppermute(block, 'rows', pairs)]
    all_gather x1 -> x0, blocking collectives: 5.64 us -> none  [body(): mid_grad = lax.all_gather(pooled, 'rows', axis=1, tiled=True)]
    unnamed x21 -> x8, local copies, waits for them, and re-layouts: 5.82 us -> 1.28 us
  transfers between devices with their start and end apart: 5 -> 8, of which waited for: 5 -> 5; matrix products, arithmetic and copies ran while one was open for 5% -> 4% of each run, Pallas kernels for 0% -> 7%
where the time goes in v2:
time: 72.7 us; the launch traced here: 72.3 us
  blocking collectives  20.1 us (28%)
  waiting for transfers between devices  18 us (25%)
  Pallas kernels  13.9 us (19%)
  starting transfers between devices  12.1 us (17%)
  other arithmetic  5.38 us (7%)
  local copies, waits for them, and re-layouts  2.01 us (3%)
    all_to_all x1, blocking collectives, work(): lax.all_to_all(packed, 'dp', 0, 0, tiled=True, axis_index_groups=groups)  20.1 us
    ppermute x1, waiting for transfers between devices, work(): moved = lax.ppermute(block, 'rows', pairs)  8.32 us
    pallas_call x1, Pallas kernels, work(): pl.pallas_call(weight_kernel(width, chips, tall, sub), out_shape=halves i...  4.84 us
    pallas_call x1, Pallas kernels, work(): pl.pallas_call(level_kernel(width), out_shape=(shape((strip + 2) * width,...  4.18 us
    ppermute x1, waiting for transfers between devices, work(): blocks = (pooled, lax.ppermute(pooled, 'rows', swap))  4.1 us
    all_to_all x1, starting transfers between devices, work(): lax.all_to_all(part, 'dp', 0, 0, tiled=True, axis_index_groups=groups)  3.64 us
    all_to_all x1, waiting for transfers between devices, work(): lax.all_to_all(part, 'dp', 0, 0, tiled=True, axis_index_groups=groups)  3.57 us
    ppermute x1, starting transfers between devices, work(): lax.ppermute(jnp.where(row == 0, low_line, top_line), 'rows', swap)  3 us
  transfers between devices with their start and end apart: 8, of which 5 were waited for; matrix products, arithmetic and copies ran while one was open for 4% of the time, Pallas kernels for 7%

profile of v2, /device:TPU:0, one launch (start us, length us, event | category | flops | bytes accessed | tf_op | source)
XLA Modules:
  0.0 72.3 jit_solution(7006459253529235667)
XLA Ops:
  0.6 0.8 %select_bitcast_fusion = bf16[64,256]{1,0:T(8,128)(2,1)S(1)} fusion(bf16[1,16,64,256]{3,2,1,0:T(8,128)(2,1)} %param.10, pred[]{:T(512)S(6)} %eq.10), kind=kLoop, calls=%fused_computation.17 | loop fusion | flops 16384 | bytes 98305 | tf_op jit(solution)/shard_map/jit(_where)/select_n | solution.py:181
  1.4 3.0 %collective-permute-start = (bf16[64,256]{1,0:T(8,128)(2,1)S(1)}, bf16[64,256]{1,0:T(8,128)(2,1)S(1)}, u32[]{:S(2)}, u32[]{:S(2)}) collective-permute-start(bf16[64,256]{1,0:T(8,128)(2,1)S(1)} %select_bitcast_fusion), channel_id=1, source_target_pairs={{0,1},{1,0},{2,3},{3,2},{4,5},{5,4},{6,7},{7,6},{8,9},{9,8},{10,11... | collective-permute-start | bytes 98312 | tf_op jit(solution)/shard_map/ppermute | solution.py:181
  4.4 0.6 pad_add_fusion.place
  5.0 1.3 %collective-permute-done.before.after = bf16[64,256]{1,0:T(8,128)(2,1)S(1)} collective-permute-done((bf16[64,256]{1,0:T(8,128)(2,1)S(1)}, bf16[64,256]{1,0:T(8,128)(2,1)S(1)}, u32[]{:S(2)}, u32[]{:S(2)}) %collective-permute-start) | collective-permute-done | bytes 32800 | tf_op jit(solution)/shard_map/ppermute | solution.py:181
  6.3 0.6 copy-done.3
  6.9 4.2 %level.1 = (bf16[1152,768]{1,0:T(8,128)(2,1)}, bf16[1024,256]{1,0:T(8,128)(2,1)}, bf16[256,256]{1,0:T(8,128)(2,1)}) custom-call(s32[4]{0:T(128)} %pad_add_fusion.place, bf16[64,256]{1,0:T(8,128)(2,1)} %copy-done.3, bf16[1024,256]{1,0:T(8,128)(2,1)} %bitcast.33, bf16[64,256]{1,0:T(8,128)(2,1)} %copy-done.3, bf16[3,3,256,256]{3,2,1,0:T(8,128)(2,1)} %weight.1), custom_call_target="tpu_custom_call" | custom-call | flops 1207959552 | tf_op jit(solution)/shard_map/level/pallas_call | solution.py:187
  11.1 4.8 %weights.1 = (f32[1280,256]{1,0:T(8,128)}, bf16[1280,256]{1,0:T(8,128)(2,1)}) custom-call(s32[4]{0:T(128)} %pad_add_fusion.place, bf16[1152,768]{1,0:T(8,128)(2,1)} %get-tuple-element.25.taps, bf16[1024,256]{1,0:T(8,128)(2,1)} %get-tuple-element.18.fine, bf16[1024,256]{1,0:T(8,128)(2,1)} %bitcast.34, bf16[1024,256]{1,0:T(8,128)(2,1)} %bitcast.35), custom_call_target="tpu_custom_call" | custom-call | flops 1342177280 | tf_op jit(solution)/shard_map/weights/pallas_call | solution.py:212
  15.9 0.0 collective-permute-start.2
  16.0 2.1 %collective-permute-start.1 = (bf16[256,256]{1,0:T(8,128)(2,1)S(1)}, bf16[256,256]{1,0:T(8,128)(2,1)S(1)}, u32[]{:S(2)}, u32[]{:S(2)}) collective-permute-start(bf16[256,256]{1,0:T(8,128)(2,1)S(1)} %copy-done.1), channel_id=1, source_target_pairs={{0,1},{1,0},{2,3},{3,2},{4,5},{5,4},{6,7},{7,6},{8,9},{9,8},{10,11... | collective-permute-start | bytes 393224 | tf_op jit(solution)/shard_map/ppermute | solution.py:202
  18.0 4.1 %collective-permute-done.1.refs_1_ = bf16[256,256]{1,0:T(8,128)(2,1)S(1)} collective-permute-done((bf16[256,256]{1,0:T(8,128)(2,1)S(1)}, bf16[256,256]{1,0:T(8,128)(2,1)S(1)}, u32[]{:S(2)}, u32[]{:S(2)}) %collective-permute-start.1) | collective-permute-done | bytes 131104 | tf_op jit(solution)/shard_map/ppermute | solution.py:202
  22.1 0.7 copy-done.2
  22.8 2.3 %coarse.1 = (bf16[512,256]{1,0:T(8,128)(2,1)}, bf16[128,256]{1,0:T(8,128)(2,1)}, f32[384,256]{1,0:T(8,128)}, bf16[384,256]{1,0:T(8,128)(2,1)}) custom-call(s32[4]{0:T(128)} %pad_add_fusion.place, bf16[256,256]{1,0:T(8,128)(2,1)} %get-tuple-element.19.refs_0_, bf16[256,256]{1,0:T(8,128)(2,1)} %copy-done.2, bf16[512,256]{1,0:T(8,128)(2,1)} %bitcast.31, ...), custom_call_target="tpu_custom_call" | custom-call | flops 100663296 | tf_op jit(solution)/shard_map/coarse/pallas_call | solution.py:246
  25.1 0.0 collective-permute-start.4
  25.1 0.0 collective-permute-done.2
  25.1 0.0 copy-start
  25.1 1.5 %convert_add_fusion = f32[1280,256]{1,0:T(8,128)S(1)} fusion(f32[1280,256]{1,0:T(8,128)} %get-tuple-element.26, bf16[1280,256]{1,0:T(8,128)(2,1)S(1)} %collective-permute-done.2), kind=kLoop, calls=%fused_computation | loop fusion | flops 655360 | bytes 3276800 | tf_op jit(solution)/shard_map/add | solution.py:235
  26.7 1.8 %collective-permute-start.3 = (bf16[640,256]{1,0:T(8,128)(2,1)S(1)}, bf16[640,256]{1,0:T(8,128)(2,1)S(1)}, u32[]{:S(2)}, u32[]{:S(2)}) collective-permute-start(bf16[640,256]{1,0:T(8,128)(2,1)S(1)} %fusion.1), channel_id=1, source_target_pairs={{0,1},{1,0},{2,3},{3,2},{4,5},{5,4},{6,7},{7,6},{8,9},{9,8},{10,11... | collective-permute-start | bytes 983048 | tf_op jit(solution)/shard_map/ppermute | solution.py:240
  28.5 0.0 collective-permute-done.4
  28.5 8.3 %collective-permute-done.3 = bf16[640,256]{1,0:T(8,128)(2,1)S(1)} collective-permute-done((bf16[640,256]{1,0:T(8,128)(2,1)S(1)}, bf16[640,256]{1,0:T(8,128)(2,1)S(1)}, u32[]{:S(2)}, u32[]{:S(2)}) %collective-permute-start.3) | collective-permute-done | bytes 327712 | tf_op jit(solution)/shard_map/ppermute | solution.py:240
  36.9 0.1 fusion
  37.0 20.1 %all_to_all.10 = bf16[8,128,256]{2,1,0:T(8,128)(2,1)S(1)} all-to-all(bf16[8,128,256]{2,1,0:T(8,128)(2,1)S(1)} %pad_maximum_fusion), channel_id=1, replica_groups={{0,4,8,12,16,20,24,28},{2,6,10,14,18,22,26,30},{1,5,9,13,17,21,25,29},{..., dimensions={0} | all-to-all | bytes 1048576 | tf_op jit(solution)/shard_map/all_to_all | solution.py:288
  57.1 0.7 broadcast_in_dim.2
  57.8 3.6 %all-to-all-start.1 = ((bf16[8,48,256]{2,1,0:T(8,128)(2,1)}), bf16[8,48,256]{2,1,0:T(8,128)(2,1)S(1)}, u32[]{:S(2)}, u32[]{:S(2)}) async-start(bf16[8,48,256]{2,1,0:T(8,128)(2,1)} %broadcast_in_dim.2), calls=%async_computation.1 | async-start | bytes 393216 | tf_op jit(solution)/shard_map/all_to_all | solution.py:298
  61.5 1.6 %collective-permute-start.5 = (f32[80,256]{1,0:T(8,128)S(1)}, f32[80,256]{1,0:T(8,128)S(1)}, u32[]{:S(2)}, u32[]{:S(2)}) collective-permute-start(f32[80,256]{1,0:T(8,128)S(1)} %convert_reduce_fusion), channel_id=1, source_target_pairs={{0,1},{1,0},{2,3},{3,2},{4,5},{5,4},{6,7},{7,6},{8,9},{9,8},{10,11... | collective-permute-start | bytes 245768 | tf_op jit(solution)/shard_map/ppermute | solution.py:293
  63.1 2.6 %grads.1 = (bf16[1024,256]{1,0:T(8,128)(2,1)}, bf16[512,256]{1,0:T(8,128)(2,1)}, bf16[128,512]{1,0:T(8,128)(2,1)}) custom-call(bf16[1024,256]{1,0:T(8,128)(2,1)} %get-tuple-element.18.fine, bf16[512,256]{1,0:T(8,128)(2,1)} %get-tuple-element.20.mid, bf16[128,256]{1,0:T(8,128)(2,1)} %get-tuple-element.21.top, bf16[256,256]{1,0:T(8,128)(2,1)} %fine_lat.1, ...), custom_call_target="tpu_custom_call" | custom-call | flops 268435456 | tf_op jit(solution)/shard_map/grads/pallas_call | solution.py:266
  65.7 3.6 %all-to-all-done.1 = bf16[8,48,256]{2,1,0:T(8,128)(2,1)S(1)} async-done(((bf16[8,48,256]{2,1,0:T(8,128)(2,1)}), bf16[8,48,256]{2,1,0:T(8,128)(2,1)S(1)}, u32[]{:S(2)}, u32[]{:S(2)}) %all-to-all-start.1) | async-done | bytes 196640 | tf_op jit(solution)/shard_map/all_to_all | solution.py:298
  69.2 0.0 collective-permute-start.6
  69.2 0.0 collective-permute-done.5
  69.3 0.7 pad_maximum_fusion.2
  70.0 0.7 %collective-permute-done.6 = bf16[384,256]{1,0:T(8,128)(2,1)S(1)} collective-permute-done((bf16[384,256]{1,0:T(8,128)(2,1)S(1)}, bf16[384,256]{1,0:T(8,128)(2,1)S(1)}, u32[]{:S(2)}, u32[]{:S(2)}) %collective-permute-start.6) | collective-permute-done | bytes 196640 | tf_op jit(solution)/shard_map/ppermute | solution.py:170
  70.7 0.8 %fusion.2 = f32[512,256]{1,0:T(8,128)} fusion(bf16[384,256]{1,0:T(8,128)(2,1)S(1)} %get-tuple-element.31, bf16[384,256]{1,0:T(8,128)(2,1)S(1)} %get-tuple-element.30), kind=kLoop, calls=%fused_computation.9 | loop fusion | flops 524288 | bytes 917504 | tf_op jit(solution)/shard_map/convert_element_type | solution.py:300
  71.6 0.7 maximum_convert_fusion
  (12 shorter events, 0.3 us)
Async XLA Ops:
  1.4 4.9 %collective-permute-start = (bf16[64,256]{1,0:T(8,128)(2,1)S(1)}, bf16[64,256]{1,0:T(8,128)(2,1)S(1)}, u32[]{:S(2)}, u32[]{:S(2)}) collective-permute-start(bf16[64,256]{1,0:T(8,128)(2,1)S(1)} %select_bitcast_fusion), channel_id=1, source_target_pairs={{0,1},{1,0},{2,3},{3,2},{4,5},{5,4},{6,7},{7,6},{8,9},{9,8},{10,11... | collective-permute-start | bytes 98312 | tf_op jit(solution)/shard_map/ppermute | solution.py:181
  6.3 0.6 copy-start.3
  11.1 4.8 %copy-start.1 = (bf16[256,256]{1,0:T(8,128)(2,1)S(1)}, bf16[256,256]{1,0:T(8,128)(2,1)}, u32[]{:S(2)}) copy-start(bf16[256,256]{1,0:T(8,128)(2,1)} %get-tuple-element.19.refs_0_) | copy-start | bytes 393220
  15.9 9.2 %collective-permute-start.2 = (bf16[1280,256]{1,0:T(8,128)(2,1)}, bf16[1280,256]{1,0:T(8,128)(2,1)S(1)}, u32[]{:S(2)}, u32[]{:S(2)}) collective-permute-start(bf16[1280,256]{1,0:T(8,128)(2,1)} %get-tuple-element.27), channel_id=1, source_target_pairs={{0,2},{2,0},{4,6},{6,4},{8,10},{10,8},{12,14},{14,12},{16,18},{18,... | collective-permute-start | bytes 1966088 | tf_op jit(solution)/shard_map/ppermute | solution.py:170
  16.0 6.2 %collective-permute-start.1 = (bf16[256,256]{1,0:T(8,128)(2,1)S(1)}, bf16[256,256]{1,0:T(8,128)(2,1)S(1)}, u32[]{:S(2)}, u32[]{:S(2)}) collective-permute-start(bf16[256,256]{1,0:T(8,128)(2,1)S(1)} %copy-done.1), channel_id=1, source_target_pairs={{0,1},{1,0},{2,3},{3,2},{4,5},{5,4},{6,7},{7,6},{8,9},{9,8},{10,11... | collective-permute-start | bytes 393224 | tf_op jit(solution)/shard_map/ppermute | solution.py:202
  22.1 0.7 copy-start.2
  25.1 3.4 %collective-permute-start.4 = (bf16[384,256]{1,0:T(8,128)(2,1)}, bf16[384,256]{1,0:T(8,128)(2,1)S(1)}, u32[]{:S(2)}, u32[]{:S(2)}) collective-permute-start(bf16[384,256]{1,0:T(8,128)(2,1)} %get-tuple-element.29), channel_id=1, source_target_pairs={{0,2},{2,0},{4,6},{6,4},{8,10},{10,8},{12,14},{14,12},{16,18},{18,... | collective-permute-start | bytes 589832 | tf_op jit(solution)/shard_map/ppermute | solution.py:170
  25.1 3.4 %copy-start = (f32[384,256]{1,0:T(8,128)S(1)}, f32[384,256]{1,0:T(8,128)}, u32[]{:S(2)}) copy-start(f32[384,256]{1,0:T(8,128)} %get-tuple-element.28) | copy-start | bytes 1179652
  26.7 10.2 %collective-permute-start.3 = (bf16[640,256]{1,0:T(8,128)(2,1)S(1)}, bf16[640,256]{1,0:T(8,128)(2,1)S(1)}, u32[]{:S(2)}, u32[]{:S(2)}) collective-permute-start(bf16[640,256]{1,0:T(8,128)(2,1)S(1)} %fusion.1), channel_id=1, source_target_pairs={{0,1},{1,0},{2,3},{3,2},{4,5},{5,4},{6,7},{7,6},{8,9},{9,8},{10,11... | collective-permute-start | bytes 983048 | tf_op jit(solution)/shard_map/ppermute | solution.py:240
  57.8 11.4 %all-to-all-start.1 = ((bf16[8,48,256]{2,1,0:T(8,128)(2,1)}), bf16[8,48,256]{2,1,0:T(8,128)(2,1)S(1)}, u32[]{:S(2)}, u32[]{:S(2)}) async-start(bf16[8,48,256]{2,1,0:T(8,128)(2,1)} %broadcast_in_dim.2), calls=%async_computation.1 | async-start | bytes 393216 | tf_op jit(solution)/shard_map/all_to_all | solution.py:298
  61.5 7.7 %collective-permute-start.5 = (f32[80,256]{1,0:T(8,128)S(1)}, f32[80,256]{1,0:T(8,128)S(1)}, u32[]{:S(2)}, u32[]{:S(2)}) collective-permute-start(f32[80,256]{1,0:T(8,128)S(1)} %convert_reduce_fusion), channel_id=1, source_target_pairs={{0,1},{1,0},{2,3},{3,2},{4,5},{5,4},{6,7},{7,6},{8,9},{9,8},{10,11... | collective-permute-start | bytes 245768 | tf_op jit(solution)/shard_map/ppermute | solution.py:293
  69.2 1.4 %collective-permute-start.6 = (bf16[384,256]{1,0:T(8,128)(2,1)S(1)}, bf16[384,256]{1,0:T(8,128)(2,1)S(1)}, u32[]{:S(2)}, u32[]{:S(2)}) collective-permute-start(bf16[384,256]{1,0:T(8,128)(2,1)S(1)} %bitcast.30), channel_id=1, source_target_pairs={{0,2},{2,0},{4,6},{6,4},{8,10},{10,8},{12,14},{14,12},{16,18},{18,... | collective-permute-start | bytes 589832 | tf_op jit(solution)/shard_map/ppermute | solution.py:170

commit v3 on v2

--- a/solution.py
+++ b/solution.py
@@ -129,6 +129,15 @@
     return run
 
 
+def finish_kernel(place, mine, other, mids, tops):
+    own, far = mine[...].astype(F32), other[...].astype(F32)
+    first = place[0] == 0
+    whole = jnp.concatenate([jnp.where(first, own, far), jnp.where(first, far, own)], axis=0)
+    count = mids.shape[0]
+    mids[...] = whole[:count]
+    tops[...] = whole[count:]
+
+
 def shape(*dims, dtype=BF):
     return jax.ShapeDtypeStruct(dims, dtype)
 
@@ -232,10 +241,14 @@
         keep, send = pick(term, core), pick(term, 1 - core).astype(BF)
     got = swap_core(send)
 
-    both = (keep + got.astype(F32)).reshape(tall, chips * sub, chans)
-    fine_sum = pick(both, row)
+    keep, got = (value.reshape(tall, chips * sub, chans) for value in (keep, got))
+
+    def pair_sum(index):
+        return pick(keep, index) + pick(got, index).astype(F32)
+
+    fine_sum = pair_sum(row)
     for move in range(1, tall):
-        block = pick(both, (row + move) % tall).astype(BF)
+        block = pair_sum((row + move) % tall).astype(BF)
         pairs = [(r, (r + move) % tall) for r in range(tall)]
         moved = lax.ppermute(block, "rows", pairs)
         fine_sum = fine_sum + moved.astype(F32)
@@ -297,15 +310,21 @@
     part = jnp.broadcast_to(part[None], (chips, piece, chans))
     part = lax.all_to_all(part, "dp", 0, 0, tiled=True, axis_index_groups=groups)
     part = part.reshape(half, chans)
-    coarse = join(core, part, swap_core(part)).astype(F32)
+    midlat_grad, toplat_grad = pl.pallas_call(
+        finish_kernel,
+        out_shape=(shape(mids, chans, dtype=F32), shape(tops, chans, dtype=F32)),
+        in_specs=[SMEM, VMEM, VMEM],
+        out_specs=(VMEM,) * 2,
+        name="finish",
+    )(there, part, swap_core(part))
 
     return (
         grad_fine.reshape(fine_input.shape),
         grad_mid.reshape(mid_input.shape),
         grad_top.reshape(top_input.shape),
         kernel_grads,
-        coarse[:mids],
-        coarse[mids:],
+        midlat_grad,
+        toplat_grad,
     )
 
 

time: 72.7 us -> 73.5 us (1.011)
  Pallas kernels: 13.9 us -> 15.9 us
  other arithmetic: 5.38 us -> 3.61 us
    pallas_call x0 -> x1, Pallas kernels: none -> 1.94 us  [work(): pl.pallas_call(finish_kernel, out_shape=(shape(mids, chans, dtype=F32), s...]
    add x1 -> x0, other arithmetic: 1.49 us -> none  [work(): both = (keep + got.astype(F32)).reshape(tall, chips * sub, chans)]
    unnamed x8 -> x14, local copies, waits for them, and re-layouts: 1.28 us -> 1.98 us
where the time goes in v3:
time: 73.5 us; the launch traced here: 73 us
  blocking collectives  20.1 us (27%)
  waiting for transfers between devices  17.9 us (24%)
  Pallas kernels  15.9 us (22%)
  starting transfers between devices  12.1 us (16%)
  other arithmetic  3.61 us (5%)
  local copies, waits for them, and re-layouts  2.67 us (4%)
    all_to_all x1, blocking collectives, work(): lax.all_to_all(packed, 'dp', 0, 0, tiled=True, axis_index_groups=groups)  20.1 us
    ppermute x1, waiting for transfers between devices, work(): moved = lax.ppermute(block, 'rows', pairs)  8.27 us
    pallas_call x1, Pallas kernels, work(): pl.pallas_call(weight_kernel(width, chips, tall, sub), out_shape=halves i...  4.83 us
    pallas_call x1, Pallas kernels, work(): pl.pallas_call(level_kernel(width), out_shape=(shape((strip + 2) * width,...  4.18 us
    ppermute x1, waiting for transfers between devices, work(): blocks = (pooled, lax.ppermute(pooled, 'rows', swap))  4.1 us
    all_to_all x1, starting transfers between devices, work(): lax.all_to_all(part, 'dp', 0, 0, tiled=True, axis_index_groups=groups)  3.64 us
    all_to_all x1, waiting for transfers between devices, work(): lax.all_to_all(part, 'dp', 0, 0, tiled=True, axis_index_groups=groups)  3.57 us
    ppermute x1, starting transfers between devices, work(): lax.ppermute(jnp.where(row == 0, low_line, top_line), 'rows', swap)  3 us
  transfers between devices with their start and end apart: 8, of which 5 were waited for; matrix products, arithmetic and copies ran while one was open for 4% of the time, Pallas kernels for 7%

profile of v3, /device:TPU:0, one launch (start us, length us, event | category | flops | bytes accessed | tf_op | source)
XLA Modules:
  0.0 73.0 jit_solution(17866851167339128402)
XLA Ops:
  0.6 0.8 %select_bitcast_fusion = bf16[64,256]{1,0:T(8,128)(2,1)S(1)} fusion(bf16[1,16,64,256]{3,2,1,0:T(8,128)(2,1)} %param.10, pred[]{:T(512)S(6)} %eq.7), kind=kLoop, calls=%fused_computation.11 | loop fusion | flops 16384 | bytes 98305 | tf_op jit(solution)/shard_map/jit(_where)/select_n | solution.py:190
  1.4 3.0 %collective-permute-start = (bf16[64,256]{1,0:T(8,128)(2,1)S(1)}, bf16[64,256]{1,0:T(8,128)(2,1)S(1)}, u32[]{:S(2)}, u32[]{:S(2)}) collective-permute-start(bf16[64,256]{1,0:T(8,128)(2,1)S(1)} %select_bitcast_fusion), channel_id=1, source_target_pairs={{0,1},{1,0},{2,3},{3,2},{4,5},{5,4},{6,7},{7,6},{8,9},{9,8},{10,11... | collective-permute-start | bytes 98312 | tf_op jit(solution)/shard_map/ppermute | solution.py:190
  4.4 0.6 pad_add_fusion.place
  5.1 1.2 %collective-permute-done.before.after = bf16[64,256]{1,0:T(8,128)(2,1)S(1)} collective-permute-done((bf16[64,256]{1,0:T(8,128)(2,1)S(1)}, bf16[64,256]{1,0:T(8,128)(2,1)S(1)}, u32[]{:S(2)}, u32[]{:S(2)}) %collective-permute-start) | collective-permute-done | bytes 32800 | tf_op jit(solution)/shard_map/ppermute | solution.py:190
  6.3 0.6 copy-done.6
  6.9 4.2 %level.1 = (bf16[1152,768]{1,0:T(8,128)(2,1)}, bf16[1024,256]{1,0:T(8,128)(2,1)}, bf16[256,256]{1,0:T(8,128)(2,1)}) custom-call(s32[4]{0:T(128)} %pad_add_fusion.place, bf16[64,256]{1,0:T(8,128)(2,1)} %copy-done.6, bf16[1024,256]{1,0:T(8,128)(2,1)} %bitcast.35, bf16[64,256]{1,0:T(8,128)(2,1)} %copy-done.6, bf16[3,3,256,256]{3,2,1,0:T(8,128)(2,1)} %weight.1), custom_call_target="tpu_custom_call" | custom-call | flops 1207959552 | tf_op jit(solution)/shard_map/level/pallas_call | solution.py:196
  11.1 4.8 %weights.1 = (f32[1280,256]{1,0:T(8,128)}, bf16[1280,256]{1,0:T(8,128)(2,1)}) custom-call(s32[4]{0:T(128)} %pad_add_fusion.place, bf16[1152,768]{1,0:T(8,128)(2,1)} %get-tuple-element.27.taps, bf16[1024,256]{1,0:T(8,128)(2,1)} %get-tuple-element.20.fine, bf16[1024,256]{1,0:T(8,128)(2,1)} %bitcast.36, bf16[1024,256]{1,0:T(8,128)(2,1)} %bitcast.37), custom_call_target="tpu_custom_call" | custom-call | flops 1342177280 | tf_op jit(solution)/shard_map/weights/pallas_call | solution.py:221
  15.9 0.0 collective-permute-start.2
  15.9 0.0 copy-done.4
  15.9 2.1 %collective-permute-start.1 = (bf16[256,256]{1,0:T(8,128)(2,1)S(1)}, bf16[256,256]{1,0:T(8,128)(2,1)S(1)}, u32[]{:S(2)}, u32[]{:S(2)}) collective-permute-start(bf16[256,256]{1,0:T(8,128)(2,1)S(1)} %copy-done.4), channel_id=1, source_target_pairs={{0,1},{1,0},{2,3},{3,2},{4,5},{5,4},{6,7},{7,6},{8,9},{9,8},{10,11... | collective-permute-start | bytes 393224 | tf_op jit(solution)/shard_map/ppermute | solution.py:211
  18.0 4.1 %collective-permute-done.1.refs_1_ = bf16[256,256]{1,0:T(8,128)(2,1)S(1)} collective-permute-done((bf16[256,256]{1,0:T(8,128)(2,1)S(1)}, bf16[256,256]{1,0:T(8,128)(2,1)S(1)}, u32[]{:S(2)}, u32[]{:S(2)}) %collective-permute-start.1) | collective-permute-done | bytes 131104 | tf_op jit(solution)/shard_map/ppermute | solution.py:211
  22.1 0.7 copy-done.5
  22.8 2.4 %coarse.1 = (bf16[512,256]{1,0:T(8,128)(2,1)}, bf16[128,256]{1,0:T(8,128)(2,1)}, f32[384,256]{1,0:T(8,128)}, bf16[384,256]{1,0:T(8,128)(2,1)}) custom-call(s32[4]{0:T(128)} %pad_add_fusion.place, bf16[256,256]{1,0:T(8,128)(2,1)} %get-tuple-element.21.refs_0_, bf16[256,256]{1,0:T(8,128)(2,1)} %copy-done.5, bf16[512,256]{1,0:T(8,128)(2,1)} %bitcast.33, ...), custom_call_target="tpu_custom_call" | custom-call | flops 100663296 | tf_op jit(solution)/shard_map/coarse/pallas_call | solution.py:259
  25.2 0.0 collective-permute-start.4
  25.2 0.0 collective-permute-done.2
  25.2 1.2 %fusion.1 = bf16[640,256]{1,0:T(8,128)(2,1)S(1)} fusion(f32[2,640,256]{2,1,0:T(8,128)} %bitcast.25, s32[]{:T(128)S(6)} %select_n.51, bf16[2,640,256]{2,1,0:T(8,128)(2,1)S(1)} %bitcast.31), kind=kLoop, calls=%fused_computation.6 | loop fusion | flops 491520 | bytes 1310724 | tf_op jit(solution)/shard_map/convert_element_type | solution.py:251
  26.4 1.8 %collective-permute-start.3 = (bf16[640,256]{1,0:T(8,128)(2,1)S(1)}, bf16[640,256]{1,0:T(8,128)(2,1)S(1)}, u32[]{:S(2)}, u32[]{:S(2)}) collective-permute-start(bf16[640,256]{1,0:T(8,128)(2,1)S(1)} %fusion.1), channel_id=1, source_target_pairs={{0,1},{1,0},{2,3},{3,2},{4,5},{5,4},{6,7},{7,6},{8,9},{9,8},{10,11... | collective-permute-start | bytes 983048 | tf_op jit(solution)/shard_map/ppermute | solution.py:253
  28.2 0.0 collective-permute-done.4
  28.3 8.3 %collective-permute-done.3 = bf16[640,256]{1,0:T(8,128)(2,1)S(1)} collective-permute-done((bf16[640,256]{1,0:T(8,128)(2,1)S(1)}, bf16[640,256]{1,0:T(8,128)(2,1)S(1)}, u32[]{:S(2)}, u32[]{:S(2)}) %collective-permute-start.3) | collective-permute-done | bytes 327712 | tf_op jit(solution)/shard_map/ppermute | solution.py:253
  36.6 0.1 fusion
  36.7 20.1 %all_to_all.10 = bf16[8,128,256]{2,1,0:T(8,128)(2,1)S(1)} all-to-all(bf16[8,128,256]{2,1,0:T(8,128)(2,1)S(1)} %pad_maximum_fusion), channel_id=1, replica_groups={{0,4,8,12,16,20,24,28},{2,6,10,14,18,22,26,30},{1,5,9,13,17,21,25,29},{..., dimensions={0} | all-to-all | bytes 1048576 | tf_op jit(solution)/shard_map/all_to_all | solution.py:301
  56.8 0.7 broadcast_in_dim.2
  57.5 3.6 %all-to-all-start.1 = ((bf16[8,48,256]{2,1,0:T(8,128)(2,1)}), bf16[8,48,256]{2,1,0:T(8,128)(2,1)S(1)}, u32[]{:S(2)}, u32[]{:S(2)}) async-start(bf16[8,48,256]{2,1,0:T(8,128)(2,1)} %broadcast_in_dim.2), calls=%async_computation.1 | async-start | bytes 393216 | tf_op jit(solution)/shard_map/all_to_all | solution.py:311
  61.2 1.6 %collective-permute-start.5 = (f32[80,256]{1,0:T(8,128)S(1)}, f32[80,256]{1,0:T(8,128)S(1)}, u32[]{:S(2)}, u32[]{:S(2)}) collective-permute-start(f32[80,256]{1,0:T(8,128)S(1)} %convert_reduce_fusion), channel_id=1, source_target_pairs={{0,1},{1,0},{2,3},{3,2},{4,5},{5,4},{6,7},{7,6},{8,9},{9,8},{10,11... | collective-permute-start | bytes 245768 | tf_op jit(solution)/shard_map/ppermute | solution.py:306
  62.8 2.6 %grads.1 = (bf16[1024,256]{1,0:T(8,128)(2,1)}, bf16[512,256]{1,0:T(8,128)(2,1)}, bf16[128,512]{1,0:T(8,128)(2,1)}) custom-call(bf16[1024,256]{1,0:T(8,128)(2,1)} %get-tuple-element.20.fine, bf16[512,256]{1,0:T(8,128)(2,1)} %get-tuple-element.22.mid, bf16[128,256]{1,0:T(8,128)(2,1)} %get-tuple-element.23.top, bf16[256,256]{1,0:T(8,128)(2,1)} %fine_lat.1, ...), custom_call_target="tpu_custom_call" | custom-call | flops 268435456 | tf_op jit(solution)/shard_map/grads/pallas_call | solution.py:279
  65.4 3.6 %all-to-all-done.1 = bf16[8,48,256]{2,1,0:T(8,128)(2,1)S(1)} async-done(((bf16[8,48,256]{2,1,0:T(8,128)(2,1)}), bf16[8,48,256]{2,1,0:T(8,128)(2,1)S(1)}, u32[]{:S(2)}, u32[]{:S(2)}) %all-to-all-start.1) | async-done | bytes 196640 | tf_op jit(solution)/shard_map/all_to_all | solution.py:311
  68.9 0.0 collective-permute-start.6
  68.9 0.0 collective-permute-done.5
  69.0 0.7 pad_maximum_fusion.1
  69.7 0.7 collective-permute-done.6.other
  70.4 0.7 copy-done.3
  71.1 1.9 %finish.1 = (f32[256,256]{1,0:T(8,128)}, f32[512,256]{1,0:T(8,128)}) custom-call(s32[4]{0:T(128)} %pad_add_fusion.place, bf16[384,256]{1,0:T(8,128)(2,1)} %bitcast.29, bf16[384,256]{1,0:T(8,128)(2,1)} %copy-done.3), custom_call_target="tpu_custom_call" | custom-call | tf_op jit(solution)/shard_map/finish/pallas_call | solution.py:313
  (15 shorter events, 0.2 us)
Async XLA Ops:
  1.4 4.9 %collective-permute-start = (bf16[64,256]{1,0:T(8,128)(2,1)S(1)}, bf16[64,256]{1,0:T(8,128)(2,1)S(1)}, u32[]{:S(2)}, u32[]{:S(2)}) collective-permute-start(bf16[64,256]{1,0:T(8,128)(2,1)S(1)} %select_bitcast_fusion), channel_id=1, source_target_pairs={{0,1},{1,0},{2,3},{3,2},{4,5},{5,4},{6,7},{7,6},{8,9},{9,8},{10,11... | collective-permute-start | bytes 98312 | tf_op jit(solution)/shard_map/ppermute | solution.py:190
  6.3 0.6 copy-start.6
  11.1 4.8 %copy-start.4 = (bf16[256,256]{1,0:T(8,128)(2,1)S(1)}, bf16[256,256]{1,0:T(8,128)(2,1)}, u32[]{:S(2)}) copy-start(bf16[256,256]{1,0:T(8,128)(2,1)} %get-tuple-element.21.refs_0_) | copy-start | bytes 393220
  15.9 9.3 %collective-permute-start.2 = (bf16[1280,256]{1,0:T(8,128)(2,1)}, bf16[1280,256]{1,0:T(8,128)(2,1)S(1)}, u32[]{:S(2)}, u32[]{:S(2)}) collective-permute-start(bf16[1280,256]{1,0:T(8,128)(2,1)} %get-tuple-element.29), channel_id=1, source_target_pairs={{0,2},{2,0},{4,6},{6,4},{8,10},{10,8},{12,14},{14,12},{16,18},{18,... | collective-permute-start | bytes 1966088 | tf_op jit(solution)/shard_map/ppermute | solution.py:179
  15.9 6.2 %collective-permute-start.1 = (bf16[256,256]{1,0:T(8,128)(2,1)S(1)}, bf16[256,256]{1,0:T(8,128)(2,1)S(1)}, u32[]{:S(2)}, u32[]{:S(2)}) collective-permute-start(bf16[256,256]{1,0:T(8,128)(2,1)S(1)} %copy-done.4), channel_id=1, source_target_pairs={{0,1},{1,0},{2,3},{3,2},{4,5},{5,4},{6,7},{7,6},{8,9},{9,8},{10,11... | collective-permute-start | bytes 393224 | tf_op jit(solution)/shard_map/ppermute | solution.py:211
  22.1 0.7 copy-start.5
  22.8 13.8 %copy-start = (f32[1280,256]{1,0:T(8,128)S(1)}, f32[1280,256]{1,0:T(8,128)}, u32[]{:S(2)}) copy-start(f32[1280,256]{1,0:T(8,128)} %get-tuple-element.28) | copy-start | bytes 3932164
  25.2 3.0 %copy-start.2 = (f32[384,256]{1,0:T(8,128)S(1)}, f32[384,256]{1,0:T(8,128)}, u32[]{:S(2)}) copy-start(f32[384,256]{1,0:T(8,128)} %get-tuple-element.30) | copy-start | bytes 1179652
  25.2 3.0 %collective-permute-start.4 = (bf16[384,256]{1,0:T(8,128)(2,1)}, bf16[384,256]{1,0:T(8,128)(2,1)S(1)}, u32[]{:S(2)}, u32[]{:S(2)}) collective-permute-start(bf16[384,256]{1,0:T(8,128)(2,1)} %get-tuple-element.31), channel_id=1, source_target_pairs={{0,2},{2,0},{4,6},{6,4},{8,10},{10,8},{12,14},{14,12},{16,18},{18,... | collective-permute-start | bytes 589832 | tf_op jit(solution)/shard_map/ppermute | solution.py:179
  26.4 10.1 %collective-permute-start.3 = (bf16[640,256]{1,0:T(8,128)(2,1)S(1)}, bf16[640,256]{1,0:T(8,128)(2,1)S(1)}, u32[]{:S(2)}, u32[]{:S(2)}) collective-permute-start(bf16[640,256]{1,0:T(8,128)(2,1)S(1)} %fusion.1), channel_id=1, source_target_pairs={{0,1},{1,0},{2,3},{3,2},{4,5},{5,4},{6,7},{7,6},{8,9},{9,8},{10,11... | collective-permute-start | bytes 983048 | tf_op jit(solution)/shard_map/ppermute | solution.py:253
  57.5 11.4 %all-to-all-start.1 = ((bf16[8,48,256]{2,1,0:T(8,128)(2,1)}), bf16[8,48,256]{2,1,0:T(8,128)(2,1)S(1)}, u32[]{:S(2)}, u32[]{:S(2)}) async-start(bf16[8,48,256]{2,1,0:T(8,128)(2,1)} %broadcast_in_dim.2), calls=%async_computation.1 | async-start | bytes 393216 | tf_op jit(solution)/shard_map/all_to_all | solution.py:311
  61.2 7.7 %collective-permute-start.5 = (f32[80,256]{1,0:T(8,128)S(1)}, f32[80,256]{1,0:T(8,128)S(1)}, u32[]{:S(2)}, u32[]{:S(2)}) collective-permute-start(f32[80,256]{1,0:T(8,128)S(1)} %convert_reduce_fusion), channel_id=1, source_target_pairs={{0,1},{1,0},{2,3},{3,2},{4,5},{5,4},{6,7},{7,6},{8,9},{9,8},{10,11... | collective-permute-start | bytes 245768 | tf_op jit(solution)/shard_map/ppermute | solution.py:306
  68.9 1.4 %copy-start.1 = (bf16[8,48,256]{2,1,0:T(8,128)(2,1)}, bf16[8,48,256]{2,1,0:T(8,128)(2,1)S(1)}, u32[]{:S(2)}) copy-start(bf16[8,48,256]{2,1,0:T(8,128)(2,1)S(1)} %all-to-all-done.1) | copy-start | bytes 589828
  68.9 1.4 %collective-permute-start.6 = (bf16[384,256]{1,0:T(8,128)(2,1)S(1)}, bf16[384,256]{1,0:T(8,128)(2,1)S(1)}, u32[]{:S(2)}, u32[]{:S(2)}) collective-permute-start(bf16[384,256]{1,0:T(8,128)(2,1)S(1)} %bitcast.28), channel_id=1, source_target_pairs={{0,2},{2,0},{4,6},{6,4},{8,10},{10,8},{12,14},{14,12},{16,18},{18,... | collective-permute-start | bytes 589832 | tf_op jit(solution)/shard_map/ppermute | solution.py:179
  70.4 0.7 copy-start.3
